TPU v7x, 32 devices: a whole 2x2x4 slice. The times are simulated.
32 devices in a mesh: gx: 4 (over z), gy: 8 (over y, x, core).
Axes of the slice: x: 2, y: 2, z: 4, core: 2. Of those that a mesh axis runs over, the one named last changes fastest.
Arguments:
- coordinates: float32 [3, 65536], P(None, ('gx', 'gy')), may hold values from 0 to 1
- rhs: float32 [16, 65536], P(None, ('gx', 'gy')), may hold values from -70 to 70
- leaf_order: int32 [32, 2048], P(('gx', 'gy')), may hold values from 0 to 2047, each once within a row
- leaf_sizes: int32 [32], P(('gx', 'gy')), may hold values from 1 to 2048, 49152 in all
- inverse_scales: float32 [3], replicated, may hold values from 12 to 30
- noise_var: float32 [1], replicated, may hold values from 0.3 to 1
- u_factors: float32 [5, 64, 65536], P(None, None, ('gx', 'gy')), may hold values from -0.375 to 0.375
- v_factors: float32 [5, 64, 65536], P(None, None, ('gx', 'gy')), may hold values from -1 to 1
Outputs:
- solution: float32 [16, 65536], P(None, ('gx', 'gy'))
Inputs may be any that keep to these rules, and one draw needn't show every extreme that they name: `leaf_sizes`: each leaf's live points stand first in leaf order.
All inputs are finite; a program needn't handle non-finite values. No bound on the sum of `leaf_sizes` on one device may be relied on, other than what follows from the above.
Results may differ from a plain program's by a relative error of at most 0.0001.
Values sent between devices are 32-bit elements; how exact they have to be, the bound alone decides.
No kernel may reach another device: no remote copies, remote signals or barrier semaphores. Data moves between devices by JAX's collectives and lax.ppermute only.
A program may use at most 128 MiB of HBM per device.

v0:
```python
import math

import jax
import jax.numpy as jnp
from jax import lax
from jax.sharding import PartitionSpec as P

ITERS = 3


epsilon = 1e-06
sqrt_three = math.sqrt(3.0)
highest = lax.Precision.HIGHEST


def partner(value, axis, apart):
    mask = 2**apart
    pairs = [(source, source ^ mask) for source in range(lax.axis_size(axis))]
    return lax.ppermute(value, axis, pairs)


def build_kernel(scaled):
    width_all = scaled.shape[1]
    block_rows = min(512, width_all)
    pieces = []
    for start_row in range(0, width_all, block_rows):
        row_points = scaled[:, start_row : start_row + block_rows]
        differ = row_points[:, :, None] - scaled[:, None, :]
        distance = jnp.sqrt(jnp.sum(differ * differ, axis=0))
        pieces.append((1.0 + sqrt_three * distance) * jnp.exp(-sqrt_three * distance))
    return jnp.concatenate(pieces, axis=0)


def least_squares(columns, beta):
    count_cols = len(columns)
    cosines = []
    sines = []
    target = [beta] + [jnp.zeros_like(beta)] * count_cols
    upper = []
    for column_idx in range(count_cols):
        entries = list(columns[column_idx])
        for row_idx in range(column_idx):
            first_val = entries[row_idx]
            second_val = entries[row_idx + 1]
            entries[row_idx] = cosines[row_idx] * first_val + sines[row_idx] * second_val
            entries[row_idx + 1] = -sines[row_idx] * first_val + cosines[row_idx] * second_val
        first_val = entries[column_idx]
        second_val = entries[column_idx + 1]
        radius = jnp.sqrt(first_val * first_val + second_val * second_val)
        cosines.append(first_val / radius)
        sines.append(second_val / radius)
        entries[column_idx] = radius
        carried = target[column_idx]
        target[column_idx] = cosines[column_idx] * carried
        target[column_idx + 1] = -sines[column_idx] * carried
        upper.append(entries[: column_idx + 1])
    weights = [None] * count_cols
    for column_idx in reversed(range(count_cols)):
        accum = target[column_idx]
        for later_idx in range(column_idx + 1, count_cols):
            accum = accum - upper[later_idx][column_idx] * weights[later_idx]
        weights[column_idx] = accum / upper[column_idx][column_idx]
    return weights


def partner_terms(partial_value):
    levels_low = lax.axis_size("gy").bit_length() - 1
    levels_high = lax.axis_size("gx").bit_length() - 1
    found = []
    remain = partial_value
    for bit_pos in range(levels_low):
        received = partner(remain, "gy", bit_pos)
        found.append(received[0])
        remain = (remain + received)[1:]
    for bit_pos in range(levels_high):
        received = partner(remain, "gx", bit_pos)
        found.append(received[0])
        remain = (remain + received)[1:]
    return jnp.stack(found)


def per_device(
    coordinates, rhs, leaf_order, leaf_sizes, inverse_scales, noise_var, u_factors, v_factors
):
    ordering = leaf_order[0]
    leaf_len = ordering.shape[0]
    num_vectors = rhs.shape[0]
    num_levels = u_factors.shape[0]
    num_rank = u_factors.shape[1]
    scaled = coordinates[:, ordering] * inverse_scales[:, None]
    live_mask = (jnp.arange(leaf_len, dtype=jnp.int32) < leaf_sizes[0]).astype(jnp.float32)
    kernel = build_kernel(scaled)
    start = live_mask * rhs[:, ordering]
    beta = jnp.sqrt(lax.psum(jnp.sum(start * start, axis=1), ("gx", "gy")) + epsilon)
    basis = [start / beta[:, None]]
    columns = []
    for step_idx in range(ITERS):
        vector = basis[step_idx]
        nearby = jnp.dot(vector, kernel, precision=highest)
        partial_value = jnp.einsum("lri,ki->lrk", v_factors, vector, precision=highest).reshape(
            num_levels, num_rank * num_vectors
        )
        sibling = partner_terms(partial_value).reshape(num_levels, num_rank, num_vectors)
        distant = jnp.einsum("lri,lrk->ki", u_factors, sibling, precision=highest)
        image = live_mask * (nearby + noise_var[0] * vector + distant)
        stacked = jnp.stack(basis)
        products = lax.psum(
            jnp.einsum("akp,kp->ak", stacked, image, precision=highest), ("gx", "gy")
        )
        image = image - jnp.einsum("ak,akp->kp", products, stacked, precision=highest)
        column = [products[row_idx] for row_idx in range(step_idx + 1)]
        length = jnp.sqrt(lax.psum(jnp.sum(image * image, axis=1), ("gx", "gy")) + epsilon)
        column.append(length)
        columns.append(column)
        if step_idx + 1 < ITERS:
            basis.append(image / length[:, None])
    weights = least_squares(columns, beta)
    solved = weights[0][:, None] * basis[0]
    for step_idx in range(1, ITERS):
        solved = solved + weights[step_idx][:, None] * basis[step_idx]
    return jnp.zeros_like(rhs).at[:, ordering].set(solved)


def solution(mesh):
    in_specs = (
        P(None, ("gx", "gy")),
        P(None, ("gx", "gy")),
        P(("gx", "gy"), None),
        P(("gx", "gy")),
        P(),
        P(),
        P(None, None, ("gx", "gy")),
        P(None, None, ("gx", "gy")),
    )
    out_specs = P(None, ("gx", "gy"))
    return jax.shard_map(
        per_device, mesh=mesh, in_specs=in_specs, out_specs=out_specs, check_vma=False
    )
```

profile of v0, /device:TPU:0, one launch (start us, length us, event | category | flops | bytes accessed | tf_op | source)
XLA Modules:
  0.0 454.8 jit_solution(3521248476799252239)
XLA Ops:
  0.0 0.9 compare_select_fusion
  0.9 2.2 copy.35
  3.1 8.8 %gather_fusion = f32[2048,16]{1,0:T(8,128)} fusion(f32[16,2048]{0,1:T(8,128)} %copy.35, s32[2048]{0:T(1024)S(1)} %broadcast_clamp_fusion), kind=kCustom, calls=%fused_computation | custom fusion | bytes 270336 | tf_op jit(solution)/shard_map/gather | solution.py:93
  11.9 1.5 copy.36
  14.2 42.0 %psum.49 = f32[16]{0:T(128)S(1)} all-reduce(f32[16]{0:T(128)S(1)} %multiply_reduce_fusion.7), channel_id=1, replica_groups=mesh['gx'=4,'gy'=8] {'gx','gy'}, use_global_device_ids=true, to_apply=%region_1.0 | all-reduce | flops 16 | bytes 128 | tf_op jit(solution)/shard_map/psum | solution.py:94
  56.7 4.7 %convolution_bitcast_fusion.5 = f32[5,64,16]{1,2,0:T(8,128)S(1)} fusion(f32[5,64,2048]{2,1,0:T(8,128)} %param.15, f32[2048,16]{0,1:T(8,128)S(1)} %copy.36, f32[16]{0:T(128)S(1)} %add_sqrt_fusion.4, f32[2048]{0:T(1024)S(1)} %fusion.31), kind=kOutput, calls=%fused_computation.29 | convolution fusion | flops 125894656 | bytes 2781248 | tf_op jit(solution)/shard_map/lri,ki->lrk/dot_general | solution.py:100
  61.6 0.7 reshape.142
  62.3 1.4 copy.37
  63.7 8.8 %gather_fusion.1 = f32[2048,3]{1,0:T(8,128)} fusion(f32[3,2048]{0,1:T(8,128)} %copy.37, s32[2048]{0:T(1024)S(1)} %broadcast_clamp_fusion), kind=kCustom, calls=%fused_computation.1 | custom fusion | bytes 57344 | tf_op jit(solution)/shard_map/gather | solution.py:90
  72.5 1.3 multiply_bitcast_fusion
  73.8 1.0 copy-done.1
  74.8 0.8 fusion.55
  75.5 2.2 copy.39
  77.7 1.1 copy.38
  78.8 0.7 copy.40
  79.7 0.8 slice_add_fusion.5
  80.5 2.3 collective-permute-start.1
  82.9 8.4 %multiply_reduce_fusion.3 = (f32[512,2048]{1,0:T(8,128)S(1)}, f32[512,2048]{1,0:T(8,128)S(1)}, f32[512,2048]{1,0:T(8,128)S(1)}, f32[512,2048]{1,0:T(8,128)S(1)}) fusion(f32[3,2048]{1,0:T(4,128)} %copy.39, f32[3,512]{1,0:T(4,128)S(1)} %copy.38, f32[3,512]{1,0:T(4,128)} %copy.40, f32[3,512]{1,0:T(4,128)S(1)} %copy.41, f32[3,512]{1,0:T(4,128)S(1)} %copy.42), kind=kLoop, calls=%fused_computation.7 | loop fusion | flops 33554432 | bytes 16826368 | tf_op jit(solution)/shard_map/reduce_sum | solution.py:29
  91.9 6.7 %exponential_multiply_fusion = (f32[512,2048]{1,0:T(8,128)}, f32[512,2048]{1,0:T(8,128)}) fusion(f32[512,2048]{1,0:T(8,128)S(1)} %get-tuple-element.8, f32[512,2048]{1,0:T(8,128)S(1)} %get-tuple-element.7), kind=kLoop, calls=%fused_computation.8 | loop fusion | flops 8388608 | bytes 16777216 | tf_op jit(solution)/shard_map/mul | solution.py:30
  98.7 1.6 collective-permute-start.3
  100.2 6.7 %exponential_multiply_fusion.2 = (f32[512,2048]{1,0:T(8,128)}, f32[512,2048]{1,0:T(8,128)}) fusion(f32[512,2048]{1,0:T(8,128)S(1)} %get-tuple-element.6, f32[512,2048]{1,0:T(8,128)S(1)} %get-tuple-element.5), kind=kLoop, calls=%fused_computation.10 | loop fusion | flops 8388608 | bytes 16777216 | tf_op jit(solution)/shard_map/mul | solution.py:30
  107.6 1.3 collective-permute-start.4
  109.0 10.7 %fusion.9 = f32[16,2048]{1,0:T(8,128)S(1)} fusion(f32[512,2048]{1,0:T(8,128)} %get-tuple-element.26, f32[512,2048]{1,0:T(8,128)} %get-tuple-element.27, f32[512,2048]{1,0:T(8,128)} %get-tuple-element.28, f32[512,2048]{1,0:T(8,128)} %get-tuple-element.29, f32[]{:T(128)} %bitcast.193, f32[16]{0:T(128)S(1)} %copy-done.5, f32[2048,16]{0,1:T(8,128)S(1)} %copy.36, ...), kind=kOutput, calls=%fused_computation.24 | convolution fusion | flops 818085888 | bytes 17047620 | tf_op jit(solution)/shard_map/dot_general | solution.py:99
  119.7 0.8 slice.140
  120.6 1.5 multiply_reduce_fusion.4
  122.1 39.7 %psum.50 = f32[16]{0:T(128)S(1)} all-reduce(f32[16]{0:T(128)S(1)} %get-tuple-element.24), channel_id=1, replica_groups=mesh['gx'=4,'gy'=8] {'gx','gy'}, use_global_device_ids=true, to_apply=%region_6.0 | all-reduce | flops 16 | bytes 128 | tf_op jit(solution)/shard_map/psum | solution.py:107
  162.0 39.8 %psum.51 = f32[16]{0:T(128)S(1)} all-reduce(f32[16]{0:T(128)S(1)} %multiply_reduce_fusion.6), channel_id=1, replica_groups=mesh['gx'=4,'gy'=8] {'gx','gy'}, use_global_device_ids=true, to_apply=%region_8.0 | all-reduce | flops 16 | bytes 128 | tf_op jit(solution)/shard_map/psum | solution.py:112
  202.5 4.7 %convolution_bitcast_fusion.4 = f32[5,64,16]{1,2,0:T(8,128)S(1)} fusion(f32[5,64,2048]{2,1,0:T(8,128)} %param.15, f32[16,2048]{1,0:T(8,128)S(1)} %broadcast_divide_fusion.1), kind=kOutput, calls=%fused_computation.28 | convolution fusion | flops 125829120 | bytes 2772992 | tf_op jit(solution)/shard_map/lri,ki->lrk/dot_general | solution.py:100
  207.6 1.2 collective-permute-done.5
  208.8 2.3 collective-permute-start.6
  211.1 1.7 collective-permute-done.6
  212.9 2.1 collective-permute-start.7
  215.0 1.6 collective-permute-done.7
  216.7 1.7 collective-permute-start.8
  218.4 11.6 %fusion.10 = f32[16,2048]{1,0:T(8,128)S(1)} fusion(f32[16,2048]{1,0:T(8,128)S(1)} %broadcast_divide_fusion.1, f32[512,2048]{1,0:T(8,128)} %get-tuple-element.26, f32[512,2048]{1,0:T(8,128)} %get-tuple-element.27, f32[512,2048]{1,0:T(8,128)} %get-tuple-element.28, f32[512,2048]{1,0:T(8,128)} %get-tuple-element.29, f32[]{:T(128)} %bitcast.195), kind=kOutput, calls=%fused_computation.25 | convolution fusion | flops 817954816 | bytes 17039364 | tf_op jit(solution)/shard_map/dot_general | solution.py:99
  230.7 0.7 pad_maximum_fusion.11
  231.5 3.2 collective-permute-done.9
  234.8 1.4 fusion.6
  236.2 3.3 fusion.20
  239.6 38.7 %psum.52 = f32[2,16]{1,0:T(2,128)S(1)} all-reduce(f32[2,16]{1,0:T(2,128)S(1)} %bitcast.206), channel_id=1, replica_groups=mesh['gx'=4,'gy'=8] {'gx','gy'}, use_global_device_ids=true, to_apply=%region_9.0 | all-reduce | flops 32 | bytes 256 | tf_op jit(solution)/shard_map/psum | solution.py:107
  278.9 2.0 fusion.18
  281.1 41.2 %psum.53 = f32[16]{0:T(128)S(1)} all-reduce(f32[16]{0:T(128)S(1)} %multiply_reduce_fusion.5), channel_id=1, replica_groups=mesh['gx'=4,'gy'=8] {'gx','gy'}, use_global_device_ids=true, to_apply=%region_11.0 | all-reduce | flops 16 | bytes 128 | tf_op jit(solution)/shard_map/psum | solution.py:112
  322.4 4.7 %convolution_bitcast_fusion.3 = f32[5,64,16]{1,2,0:T(8,128)S(1)} fusion(f32[5,64,2048]{2,1,0:T(8,128)} %param.15, f32[16,2048]{1,0:T(8,128)S(1)} %broadcast_divide_fusion), kind=kOutput, calls=%fused_computation.27 | convolution fusion | flops 125829120 | bytes 2772992 | tf_op jit(solution)/shard_map/lri,ki->lrk/dot_general | solution.py:100
  327.5 1.2 collective-permute-done.10
  328.7 2.3 collective-permute-start.11
  331.0 1.7 collective-permute-done.11
  332.7 2.1 collective-permute-start.12
  334.8 1.7 collective-permute-done.12
  336.9 12.2 %fusion.11 = f32[16,2048]{1,0:T(8,128)} fusion(f32[16,2048]{1,0:T(8,128)S(1)} %broadcast_divide_fusion, f32[512,2048]{1,0:T(8,128)} %get-tuple-element.26, f32[512,2048]{1,0:T(8,128)} %get-tuple-element.27, f32[512,2048]{1,0:T(8,128)} %get-tuple-element.28, f32[512,2048]{1,0:T(8,128)} %get-tuple-element.29, f32[]{:T(128)} %bitcast.194), kind=kOutput, calls=%fused_computation.26 | convolution fusion | flops 817954816 | bytes 17039364 | tf_op jit(solution)/shard_map/dot_general | solution.py:99
  349.1 1.9 collective-permute-start.14
  351.1 2.6 collective-permute-done.14
  353.8 0.8 reshape.147
  354.5 2.4 fusion.4
  356.9 2.4 fusion.14
  359.3 0.7 copy.65
  360.0 40.4 %psum.54 = f32[3,16]{1,0:T(4,128)} all-reduce(f32[3,16]{1,0:T(4,128)} %bitcast.205), channel_id=1, replica_groups=mesh['gx'=4,'gy'=8] {'gx','gy'}, use_global_device_ids=true, to_apply=%region_12.0 | all-reduce | flops 48 | bytes 384 | tf_op jit(solution)/shard_map/psum | solution.py:107
  400.3 0.8 copy.66
  401.1 1.1 fusion.12
  402.4 40.0 %psum.55 = f32[16]{0:T(128)S(1)} all-reduce(f32[16]{0:T(128)S(1)} %fusion.24), channel_id=1, replica_groups=mesh['gx'=4,'gy'=8] {'gx','gy'}, use_global_device_ids=true, to_apply=%region_14.0 | all-reduce | flops 16 | bytes 128 | tf_op jit(solution)/shard_map/psum | solution.py:112
  442.4 0.9 fusion.45
  443.2 0.8 add_bitcast_fusion
  444.0 1.3 copy.49
  445.3 7.0 %scatter_custom_fusion = f32[16,2048]{0,1:T(8,128)} fusion(s32[2048]{0:T(1024)} %bitcast.202, f32[2048,16]{1,0:T(8,128)} %copy.49, f32[]{:T(128)} %constant.7.clone.1), kind=kCustom, calls=%fused_computation.35 | custom fusion | bytes 131584 | tf_op jit(solution)/shard_map/scatter | solution.py:121
  452.3 2.2 copy.50
  (82 shorter events, 5.9 us)
Async XLA Ops:
  0.0 120.6 %copy-start = (f32[5,64,2048]{2,1,0:T(8,128)S(1)}, f32[5,64,2048]{2,1,0:T(8,128)}, u32[]{:S(2)}) copy-start(f32[5,64,2048]{2,1,0:T(8,128)} %param.14) | copy-start | bytes 7864324
  0.0 62.3 %copy-start.2 = (f32[3,2048]{1,0:T(4,128)S(1)}, f32[3,2048]{1,0:T(4,128)}, u32[]{:S(2)}) copy-start(f32[3,2048]{1,0:T(4,128)} %param.8) | copy-start | bytes 73732
  0.0 72.5 %copy-start.9 = (f32[3]{0:T(128)S(1)}, f32[3]{0:T(128)}, u32[]{:S(2)}) copy-start(f32[3]{0:T(128)} %param.12) | copy-start | bytes 40
  0.9 2.3 copy-start.3
  56.2 0.5 copy-start.10
  56.7 15.8 %copy-start.4 = (f32[16]{0:T(128)}, f32[16]{0:T(128)S(1)}, u32[]{:S(2)}) copy-start(f32[16]{0:T(128)S(1)} %add_sqrt_fusion.4) | copy-start | bytes 196
  62.3 17.4 %collective-permute-start = (f32[5,1024]{1,0:T(8,128)}, f32[5,1024]{1,0:T(8,128)}, u32[]{:S(2)}, u32[]{:S(2)}) collective-permute-start(f32[5,1024]{1,0:T(8,128)} %reshape.142), channel_id=1, source_target_pairs={{0,1},{1,0},{2,3},{3,2},{4,5},{5,4},{6,7},{7,6},{8,9},{9,8},{10,11... | collective-permute-start | bytes 61448 | tf_op jit(solution)/shard_map/ppermute | solution.py:19
  73.8 1.0 copy-start.1
  80.5 10.7 %collective-permute-start.1 = (f32[4,1024]{1,0:T(4,128)S(1)}, f32[4,1024]{1,0:T(4,128)S(1)}, u32[]{:S(2)}, u32[]{:S(2)}) collective-permute-start(f32[4,1024]{1,0:T(4,128)S(1)} %slice_add_fusion.5), channel_id=1, source_target_pairs={{0,2},{1,3},{2,0},{3,1},{4,6},{5,7},{6,4},{7,5},{8,10},{9,11},{10,... | collective-permute-start | bytes 49160 | tf_op jit(solution)/shard_map/ppermute | solution.py:19
  91.3 7.4 %collective-permute-start.2 = (f32[3,1024]{1,0:T(4,128)S(1)}, f32[3,1024]{1,0:T(4,128)S(1)}, u32[]{:S(2)}, u32[]{:S(2)}) collective-permute-start(f32[3,1024]{1,0:T(4,128)S(1)} %slice_add_fusion.4), channel_id=1, source_target_pairs={{0,4},{1,5},{2,6},{3,7},{4,0},{5,1},{6,2},{7,3},{8,12},{9,13},{10,... | collective-permute-start | bytes 36872 | tf_op jit(solution)/shard_map/ppermute | solution.py:19
  98.7 9.0 %collective-permute-start.3 = (f32[2,1024]{1,0:T(2,128)S(1)}, f32[2,1024]{1,0:T(2,128)S(1)}, u32[]{:S(2)}, u32[]{:S(2)}) collective-permute-start(f32[2,1024]{1,0:T(2,128)S(1)} %slice_add_fusion.8), channel_id=1, source_target_pairs={{0,8},{8,0},{16,24},{24,16},{1,9},{9,1},{17,25},{25,17},{2,10},{10... | collective-permute-start | bytes 24584 | tf_op jit(solution)/shard_map/ppermute | solution.py:19
  100.2 8.7 %copy-start.5 = (f32[16]{0:T(128)S(1)}, f32[16]{0:T(128)}, u32[]{:S(2)}) copy-start(f32[16]{0:T(128)} %copy-done.4) | copy-start | bytes 196
  107.6 12.8 %collective-permute-start.4 = (f32[1,1024]{1,0:T(1,128)S(1)}, f32[1,1024]{1,0:T(1,128)S(1)}, u32[]{:S(2)}, u32[]{:S(2)}) collective-permute-start(f32[1,1024]{1,0:T(1,128)S(1)} %get-tuple-element.20), channel_id=1, source_target_pairs={{0,16},{8,24},{16,0},{24,8},{1,17},{9,25},{17,1},{25,9},{2,18},{10... | collective-permute-start | bytes 12296 | tf_op jit(solution)/shard_map/ppermute | solution.py:19
  161.8 68.2 %copy-start.7 = (f32[16]{0:T(128)}, f32[16]{0:T(128)S(1)}, u32[]{:S(2)}) copy-start(f32[16]{0:T(128)S(1)} %psum.50) | copy-start | bytes 196
  201.9 0.6 copy-start.8
  207.5 1.3 collective-permute-start.5
  208.8 4.1 collective-permute-start.6
  212.9 3.8 collective-permute-start.7
  216.7 13.3 %collective-permute-start.8 = (f32[2,1024]{1,0:T(2,128)S(1)}, f32[2,1024]{1,0:T(2,128)S(1)}, u32[]{:S(2)}, u32[]{:S(2)}) collective-permute-start(f32[2,1024]{1,0:T(2,128)S(1)} %slice_add_fusion.7), channel_id=1, source_target_pairs={{0,8},{8,0},{16,24},{24,16},{1,9},{9,1},{17,25},{25,17},{2,10},{10... | collective-permute-start | bytes 24584 | tf_op jit(solution)/shard_map/ppermute | solution.py:19
  230.1 4.6 %collective-permute-start.9 = (f32[1,1024]{1,0:T(1,128)S(1)}, f32[1,1024]{1,0:T(1,128)S(1)}, u32[]{:S(2)}, u32[]{:S(2)}) collective-permute-start(f32[1,1024]{1,0:T(1,128)S(1)} %get-tuple-element.18), channel_id=1, source_target_pairs={{0,16},{8,24},{16,0},{24,8},{1,17},{9,25},{17,1},{25,9},{2,18},{10... | collective-permute-start | bytes 12296 | tf_op jit(solution)/shard_map/ppermute | solution.py:19
  278.3 0.6 copy-start.6
  322.3 26.8 %copy-start.11 = (f32[16]{0:T(128)}, f32[16]{0:T(128)S(1)}, u32[]{:S(2)}) copy-start(f32[16]{0:T(128)S(1)} %psum.53) | copy-start | bytes 196
  327.4 1.3 collective-permute-start.10
  328.7 4.1 collective-permute-start.11
  332.7 3.8 collective-permute-start.12
  336.6 12.6 %collective-permute-start.13 = (f32[2,1024]{1,0:T(2,128)S(1)}, f32[2,1024]{1,0:T(2,128)S(1)}, u32[]{:S(2)}, u32[]{:S(2)}) collective-permute-start(f32[2,1024]{1,0:T(2,128)S(1)} %slice_add_fusion.6), channel_id=1, source_target_pairs={{0,8},{8,0},{16,24},{24,16},{1,9},{9,1},{17,25},{25,17},{2,10},{10... | collective-permute-start | bytes 24584 | tf_op jit(solution)/shard_map/ppermute | solution.py:19
  349.1 4.6 %collective-permute-start.14 = (f32[1,1024]{1,0:T(1,128)S(1)}, f32[1,1024]{1,0:T(1,128)S(1)}, u32[]{:S(2)}, u32[]{:S(2)}) collective-permute-start(f32[1,1024]{1,0:T(1,128)S(1)} %get-tuple-element.16), channel_id=1, source_target_pairs={{0,16},{8,24},{16,0},{24,8},{1,17},{9,25},{17,1},{25,9},{2,18},{10... | collective-permute-start | bytes 12296 | tf_op jit(solution)/shard_map/ppermute | solution.py:19
where the time goes:
time: 462 us; the launch traced here: 455 us
  blocking collectives  282 us (61%)
  matrix products  62.8 us (14%)
  local copies, waits for them, and re-layouts  45.1 us (10%)
  other arithmetic  28.8 us (6%)
  starting transfers between devices  19.5 us (4%)
  waiting for transfers between devices  15 us (3%)
    psum x3, blocking collectives, per_device(): lax.psum(jnp.sum(image * image, axis=1), ('gx', 'gy')) + epsilon  121 us
    psum x3, blocking collectives, per_device(): lax.psum(jnp.einsum('akp,kp->ak', stacked, image, precision=highest), ('g...  119 us
    psum x1, blocking collectives, per_device(): lax.psum(jnp.sum(start * start, axis=1), ('gx', 'gy')) + epsilon  42 us
    dot_general x3, matrix products, per_device(): nearby = jnp.dot(vector, kernel, precision=highest)  34.5 us
    ppermute x15, starting transfers between devices, partner(): return lax.ppermute(value, axis, pairs)  19.5 us
    ppermute x15, waiting for transfers between devices, partner(): return lax.ppermute(value, axis, pairs)  15 us
    dot_general x3, matrix products, per_device(): jnp.einsum('lri,ki->lrk', v_factors, vector, precision=highest)  14.2 us
    mul x2, other arithmetic, build_kernel(): (1.0 + sqrt_three * distance) * jnp.exp(-sqrt_three * distance)  13.5 us
  transfers between devices with their start and end apart: 15, of which 8 were waited for; matrix products, arithmetic and copies ran while one was open for 16% of the time, Pallas kernels for 0%

commit v1 on v0

v1 whole, which is shorter than its diff:
```python
import functools
import math

import jax
import jax.numpy as jnp
from jax import lax
from jax.experimental import pallas as pl
from jax.experimental.pallas import tpu as pltpu
from jax.sharding import PartitionSpec as P

AXES = ("gx", "gy")
LANES = 128
TILE = 256
EPSILON = 1e-06
DISTANCE_SCALE = math.sqrt(3.0) / math.log(2.0)
LN2 = math.log(2.0)
f32 = jnp.float32
bf16 = jnp.bfloat16


def split(x, parts):
    pieces = []
    for part in range(parts):
        piece = x.astype(bf16)
        pieces.append(piece)
        if part + 1 < parts:
            x = x - piece.astype(f32)
    return pieces


def dot(a, b):
    return lax.dot_general(a, b, (((1,), (0,)), ((), ())), preferred_element_type=f32)


def dot_nt(a, b):
    return lax.dot_general(a, b, (((1,), (1,)), ((), ())), preferred_element_type=f32)


def live_row(size, length):
    return lax.broadcasted_iota(jnp.int32, (1, length), 1) < size


def levels_of(num, levels):
    me = lax.axis_index("gx") * lax.axis_size("gy") + lax.axis_index("gy")
    apart = lax.broadcasted_iota(jnp.int32, (num, 1), 0) ^ me
    level = jnp.full((num, 1), -1, jnp.int32)
    for bit in range(levels):
        level = level + (apart >= (1 << bit)).astype(jnp.int32)
    return level


def diagonal(vectors):
    shape = (LANES // vectors, LANES)
    return lax.broadcasted_iota(jnp.int32, shape, 1) // vectors == lax.broadcasted_iota(
        jnp.int32, shape, 0
    )


def slot_mask(vectors, slot):
    shape = (vectors, LANES)
    return (
        lax.broadcasted_iota(jnp.int32, shape, 1)
        == lax.broadcasted_iota(jnp.int32, shape, 0) + slot * vectors
    )


def pack_dots(pairs, vectors):
    rows = jnp.zeros((vectors, LANES), f32)
    for slot, (a, b) in enumerate(pairs):
        total = jnp.sum(a * b, axis=1, keepdims=True)
        rows = jnp.where(slot_mask(vectors, slot), total, rows)
    return jnp.sum(rows, axis=0, keepdims=True)


def unpack_dots(received, count, vectors):
    total = jnp.sum(received, axis=0, keepdims=True)
    out = []
    for slot in range(count):
        chosen = jnp.where(slot_mask(vectors, slot), total, 0.0)
        out.append(jnp.sum(chosen, axis=1, keepdims=True))
    return out


def send_coefs(vector, high, low, pay_ref, dots, levels, rank):
    vectors = vector.shape[0]
    group = LANES // vectors
    num = pay_ref.shape[0]
    first, second = split(vector, 2)
    wide = jnp.concatenate([first] * group + [second] * group, axis=0)
    both = dot_nt(high, wide) + dot_nt(low, wide)
    both = both[:, :LANES] + both[:, LANES:]
    mask = diagonal(vectors)
    level = levels_of(num, levels)
    for block in range(rank // group):
        rows = jnp.zeros((num, LANES), f32)
        for lev in range(levels):
            start = lev * rank + block * group
            piece = jnp.where(mask, both[start : start + group], 0.0)
            rows = jnp.where(level == lev, jnp.sum(piece, axis=0, keepdims=True), rows)
        pay_ref[:, block * LANES : (block + 1) * LANES] = rows
    pay_ref[:, rank * vectors :] = jnp.broadcast_to(dots, (num, LANES))


def receive_coefs(recv_ref, vectors, levels, rank):
    num = recv_ref.shape[0]
    group = LANES // vectors
    mask = diagonal(vectors)
    level = levels_of(num, levels)
    pieces = []
    for lev in range(levels):
        for block in range(rank // group):
            part = recv_ref[:, block * LANES : (block + 1) * LANES]
            total = jnp.sum(jnp.where(level == lev, part, 0.0), axis=0, keepdims=True)
            pieces.append(jnp.where(mask, jnp.broadcast_to(total, mask.shape), 0.0))
    flipped = jnp.concatenate(pieces, axis=0).T
    out = flipped[:vectors]
    for row in range(1, group):
        out = out + flipped[row * vectors : (row + 1) * vectors]
    return out


def expand(coefs, high, low):
    vectors = coefs.shape[0]
    stacked = jnp.concatenate(split(coefs, 3), axis=0)
    out = dot(stacked, high) + dot(stacked, low)
    return out[:vectors] + out[vectors : 2 * vectors] + out[2 * vectors :]


def one_hot(row, length):
    width = row.shape[1]
    steps = lax.broadcasted_iota(jnp.int32, (TILE, width), 0).astype(f32).astype(bf16)
    pieces = []
    for base in range(0, length, TILE):
        local = (row - base).astype(f32)
        local = jnp.broadcast_to(local, (TILE, width)).astype(bf16)
        pieces.append(jnp.where(steps == local, jnp.ones((), bf16), jnp.zeros((), bf16)))
    return jnp.concatenate(pieces, axis=0)


def start_body(
    sizes_ref, scales_ref, order_ref, rhs_ref, coords_ref, v_ref,
    start_ref, points_ref, pay_ref, v1_ref, v2_ref, pad_ref, *, levels, rank,
):
    vectors, length = rhs_ref.shape
    dims = coords_ref.shape[0]
    pad_ref[...] = jnp.zeros(pad_ref.shape, f32)
    pad_ref[:dims, :] = coords_ref[...]
    stacked = jnp.concatenate(
        [p.astype(f32) for p in split(rhs_ref[...], 3)]
        + [p.astype(f32) for p in split(pad_ref[...], 3)],
        axis=0,
    ).astype(bf16)
    rows = pad_ref.shape[0]
    row_id = lax.broadcasted_iota(jnp.int32, (rows, 1), 0)
    scale = jnp.zeros((rows, 1), f32)
    for dim in range(dims):
        scale = jnp.where(row_id == dim, scales_ref[dim] * DISTANCE_SCALE, scale)
    for base in range(0, length, TILE):
        chosen = dot(stacked, one_hot(order_ref[:, base : base + TILE], length))
        lane = base + lax.broadcasted_iota(jnp.int32, (1, TILE), 1)
        value = chosen[:vectors] + chosen[vectors : 2 * vectors] + chosen[2 * vectors : 3 * vectors]
        start_ref[:, base : base + TILE] = jnp.where(lane < sizes_ref[0], value, 0.0)
        rest = chosen[3 * vectors :]
        value = rest[:rows] + rest[rows : 2 * rows] + rest[2 * rows :]
        points_ref[:, base : base + TILE] = value * scale
    high, low = split(v_ref[...], 2)
    v1_ref[...] = high
    v2_ref[...] = low
    start = start_ref[...]
    dots = pack_dots([(start, start)], vectors)
    send_coefs(start, high, low, pay_ref, dots, levels, rank)


def dense(vector, high_ref, low_ref, acc_ref):
    vectors, length = vector.shape
    stacked = jnp.concatenate(split(vector, 3), axis=0)
    offset = 0
    for base in range(0, length, TILE):
        width = length - base
        own = stacked[:, base : base + TILE]
        high = high_ref[:, offset : offset + width]
        low = low_ref[:, offset : offset + width]
        part = dot(own, high) + dot(own, low)
        if base == 0:
            acc_ref[...] = part
        else:
            acc_ref[:, base:] += part
        if width > TILE:
            rest = stacked[:, base + TILE :]
            acc_ref[:, base : base + TILE] += dot_nt(rest, high[:, TILE:]) + dot_nt(
                rest, low[:, TILE:]
            )
        offset += width
    out = acc_ref[...]
    return out[:vectors] + out[vectors : 2 * vectors] + out[2 * vectors :]


def build_body(
    noise_ref, points_ref, start_ref, u_ref, high_ref, low_ref, image_ref, u1_ref, u2_ref,
    column_ref, acc_ref, *, dims,
):
    length = points_ref.shape[1]
    step = 16
    column_ref[...] = points_ref[...].T
    high, low = split(u_ref[...], 2)
    u1_ref[...] = high
    u2_ref[...] = low
    offset = 0
    for base in range(0, length, TILE):
        width = length - base

        def rows_step(index, carry, base=base, width=width, offset=offset):
            row = pl.multiple_of(index * step, step)
            square = None
            for dim in range(dims):
                differ = (
                    column_ref[pl.ds(base + row, step), dim : dim + 1]
                    - points_ref[dim : dim + 1, base:]
                )
                square = differ * differ if square is None else square + differ * differ
            square = jnp.maximum(square, 1e-30)
            distance = square * lax.rsqrt(square)
            value = (1.0 + LN2 * distance) * jnp.exp2(-distance)
            high, low = split(value, 2)
            high_ref[pl.ds(row, step), offset : offset + width] = high
            low_ref[pl.ds(row, step), offset : offset + width] = low
            return carry

        lax.fori_loop(0, TILE // step, rows_step, 0)
        offset += width
    start = start_ref[...]
    image_ref[...] = dense(start, high_ref, low_ref, acc_ref) + noise_ref[0] * start


def dense_body(noise_ref, vector_ref, high_ref, low_ref, image_ref, acc_ref):
    vector = vector_ref[...]
    image_ref[...] = dense(vector, high_ref, low_ref, acc_ref) + noise_ref[0] * vector


def inverse_body(order_ref, inverse_ref):
    length = order_ref.shape[1]
    place = lax.broadcasted_iota(jnp.int32, (8, TILE), 1).astype(f32)
    row_id = lax.broadcasted_iota(jnp.int32, (8, TILE), 0)
    total = jnp.zeros((8, length), f32)
    for base in range(0, length, TILE):
        weights = jnp.where(row_id == 0, place, float(base // TILE))
        hot = one_hot(order_ref[:, base : base + TILE], length)
        total = total + dot_nt(weights.astype(bf16), hot)
    inverse_ref[...] = (total[0:1] + total[1:2] * float(TILE)).astype(jnp.int32)


def first_body(
    sizes_ref, recv_ref, image_ref, start_ref, u1_ref, u2_ref, v1_ref, v2_ref,
    q0_ref, w0_ref, scal_ref, pay_ref, *, levels, rank,
):
    vectors, length = start_ref.shape
    live = live_row(sizes_ref[0], length)
    (norm,) = unpack_dots(recv_ref[:, rank * vectors :], 1, vectors)
    beta = jnp.sqrt(norm + EPSILON)
    inverse = 1.0 / beta
    distant = expand(receive_coefs(recv_ref, vectors, levels, rank), u1_ref[...], u2_ref[...])
    w0 = jnp.where(live, image_ref[...] + distant, 0.0) * inverse
    q0 = start_ref[...] * inverse
    q0_ref[...] = q0
    w0_ref[...] = w0
    scal_ref[...] = jnp.broadcast_to(beta, scal_ref.shape)
    dots = pack_dots([(q0, q0), (q0, w0), (w0, w0)], vectors)
    send_coefs(w0, v1_ref[...], v2_ref[...], pay_ref, dots, levels, rank)


def put_scalars(scal_ref, values):
    lane = lax.broadcasted_iota(jnp.int32, scal_ref.shape, 1)
    out = jnp.zeros(scal_ref.shape, f32)
    for slot, value in enumerate(values):
        out = jnp.where(lane == slot, value, out)
    scal_ref[...] = out


def get_scalars(scal_ref, count):
    return [scal_ref[:, slot : slot + 1] for slot in range(count)]


def second_body(
    sizes_ref, recv_ref, image_ref, q0_ref, w0_ref, old_ref, u1_ref, u2_ref, v1_ref, v2_ref,
    q1_ref, w1_ref, scal_ref, pay_ref, *, levels, rank,
):
    vectors, length = q0_ref.shape
    live = live_row(sizes_ref[0], length)
    (beta,) = get_scalars(old_ref, 1)
    g00, h00, norm = unpack_dots(recv_ref[:, rank * vectors :], 3, vectors)
    rest = norm - 2.0 * h00 * h00 + h00 * h00 * g00
    h10 = jnp.sqrt(jnp.maximum(rest, 0.0) + EPSILON)
    inverse = 1.0 / h10
    put_scalars(scal_ref, [beta, g00, h00, h10])
    distant = expand(receive_coefs(recv_ref, vectors, levels, rank), u1_ref[...], u2_ref[...])
    w0 = w0_ref[...]
    q0 = q0_ref[...]
    q1 = (w0 - h00 * q0) * inverse
    w1 = (jnp.where(live, image_ref[...] + distant, 0.0) - h00 * w0) * inverse
    q1_ref[...] = q1
    w1_ref[...] = w1
    dots = pack_dots([(q0, w1), (q1, w1), (w1, w1), (q0, q1), (q1, q1)], vectors)
    send_coefs(w1, v1_ref[...], v2_ref[...], pay_ref, dots, levels, rank)


def third_body(
    sizes_ref, recv_ref, image_ref, q0_ref, q1_ref, w0_ref, w1_ref, old_ref, u1_ref, u2_ref,
    q2_ref, scal_ref, pay_ref, *, levels, rank,
):
    vectors, length = q0_ref.shape
    live = live_row(sizes_ref[0], length)
    beta, g00, h00, h10 = get_scalars(old_ref, 4)
    h01, h11, norm, g01, g11 = unpack_dots(recv_ref[:, rank * vectors :], 5, vectors)
    rest = (
        norm - 2.0 * (h01 * h01 + h11 * h11)
        + (h01 * h01 * g00 + h11 * h11 * g11 + 2.0 * h01 * h11 * g01)
    )
    h21 = jnp.sqrt(jnp.maximum(rest, 0.0) + EPSILON)
    inverse = 1.0 / h21
    put_scalars(scal_ref, [beta, g00, h00, h10, g01, g11, h01, h11, h21])
    distant = expand(receive_coefs(recv_ref, vectors, levels, rank), u1_ref[...], u2_ref[...])
    w0 = w0_ref[...]
    w1 = w1_ref[...]
    q0 = q0_ref[...]
    q1 = q1_ref[...]
    q2 = (w1 - h01 * q0 - h11 * q1) * inverse
    image = jnp.where(live, image_ref[...] + distant, 0.0)
    w2 = (image - h01 * w0 - h11 * w1) * inverse
    q2_ref[...] = q2
    dots = pack_dots(
        [(q0, w2), (q1, w2), (q2, w2), (w2, w2), (q0, q2), (q1, q2), (q2, q2)], vectors
    )
    pay_ref[...] = jnp.broadcast_to(dots, pay_ref.shape)


def least_squares(columns, beta):
    count_cols = len(columns)
    cosines = []
    sines = []
    target = [beta] + [jnp.zeros_like(beta)] * count_cols
    upper = []
    for column_idx in range(count_cols):
        entries = list(columns[column_idx])
        for row_idx in range(column_idx):
            first_val = entries[row_idx]
            second_val = entries[row_idx + 1]
            entries[row_idx] = cosines[row_idx] * first_val + sines[row_idx] * second_val
            entries[row_idx + 1] = -sines[row_idx] * first_val + cosines[row_idx] * second_val
        first_val = entries[column_idx]
        second_val = entries[column_idx + 1]
        radius = jnp.sqrt(first_val * first_val + second_val * second_val)
        cosines.append(first_val / radius)
        sines.append(second_val / radius)
        entries[column_idx] = radius
        carried = target[column_idx]
        target[column_idx] = cosines[column_idx] * carried
        target[column_idx + 1] = -sines[column_idx] * carried
        upper.append(entries[: column_idx + 1])
    weights = [None] * count_cols
    for column_idx in reversed(range(count_cols)):
        accum = target[column_idx]
        for later_idx in range(column_idx + 1, count_cols):
            accum = accum - upper[later_idx][column_idx] * weights[later_idx]
        weights[column_idx] = accum / upper[column_idx][column_idx]
    return weights


def last_body(recv_ref, q0_ref, q1_ref, q2_ref, old_ref, inverse_ref, out_ref):
    vectors, length = q0_ref.shape
    beta, g00, h00, h10, g01, g11, h01, h11, h21 = get_scalars(old_ref, 9)
    h02, h12, h22, norm, g02, g12, g22 = unpack_dots(recv_ref[...], 7, vectors)
    rest = (
        norm - 2.0 * (h02 * h02 + h12 * h12 + h22 * h22)
        + (h02 * h02 * g00 + h12 * h12 * g11 + h22 * h22 * g22)
        + 2.0 * (h02 * h12 * g01 + h02 * h22 * g02 + h12 * h22 * g12)
    )
    h32 = jnp.sqrt(jnp.maximum(rest, 0.0) + EPSILON)
    y0, y1, y2 = least_squares([[h00, h10], [h01, h11, h21], [h02, h12, h22, h32]], beta)
    solved = y0 * q0_ref[...] + y1 * q1_ref[...] + y2 * q2_ref[...]
    stacked = jnp.concatenate(split(solved, 3), axis=0)
    for base in range(0, length, TILE):
        placed = dot(stacked, one_hot(inverse_ref[:, base : base + TILE], length))
        out_ref[:, base : base + TILE] = (
            placed[:vectors] + placed[vectors : 2 * vectors] + placed[2 * vectors :]
        )


def call(body, outs, args, smem=0, scratch=(), flops=0, limit=20, name=None):
    smem_spec = pl.BlockSpec(memory_space=pltpu.SMEM)
    vmem_spec = pl.BlockSpec(memory_space=pltpu.VMEM)
    specs = [smem_spec] * smem + [vmem_spec] * (len(args) - smem)
    total = sum(math.prod(a.shape) * a.dtype.itemsize for a in list(args) + list(outs))
    return pl.pallas_call(
        body,
        out_shape=list(outs),
        in_specs=specs,
        out_specs=[vmem_spec] * len(outs),
        scratch_shapes=list(scratch),
        compiler_params=pltpu.CompilerParams(vmem_limit_bytes=limit * 1024 * 1024),
        cost_estimate=pl.CostEstimate(flops=flops, bytes_accessed=total, transcendentals=0),
        name=name,
    )(*args)


def exchange(payload):
    return lax.all_to_all(payload, AXES, 0, 0, tiled=True)


def per_device(
    coordinates, rhs, leaf_order, leaf_sizes, inverse_scales, noise_var, u_factors, v_factors
):
    vectors, length = rhs.shape
    dims = coordinates.shape[0]
    levels, rank, _ = u_factors.shape
    num = lax.axis_size("gx") * lax.axis_size("gy")
    blocks = length // TILE
    packed = TILE * (blocks * (blocks + 1) // 2)
    padded = -(-dims // 8) * 8
    u_flat = u_factors.reshape(levels * rank, length)
    v_flat = v_factors.reshape(levels * rank, length)

    def shaped(*shape, dtype=f32):
        return jax.ShapeDtypeStruct(shape, dtype)

    field = shaped(vectors, length)
    factor = shaped(levels * rank, length, dtype=bf16)
    scalars = shaped(vectors, LANES)
    message = shaped(num, rank * vectors + LANES)
    acc = pltpu.VMEM((3 * vectors, length), f32)
    sizes = dict(levels=levels, rank=rank)
    small = 2 * levels * rank * length * 256

    start, points, pay, v1, v2 = call(
        functools.partial(start_body, **sizes),
        [field, shaped(padded, length), message, factor, factor],
        [leaf_sizes, inverse_scales, leaf_order, rhs, coordinates, v_flat],
        smem=2, scratch=[pltpu.VMEM((padded, length), f32)], flops=small, name="start",
    )
    recv = exchange(pay)
    k1, k2, image, u1, u2 = call(
        functools.partial(build_body, dims=dims),
        [shaped(TILE, packed, dtype=bf16)] * 2 + [field, factor, factor],
        [noise_var, points, start, u_flat],
        smem=1, scratch=[pltpu.VMEM((length, padded), f32), acc],
        flops=2 * length * length * 256, limit=30, name="build",
    )
    (inverse,) = call(
        inverse_body, [shaped(1, length, dtype=jnp.int32)], [leaf_order],
        flops=2 * length * length * 64, name="inverse",
    )

    def near(vector, name):
        (out,) = call(
            dense_body, [field], [noise_var, vector, k1, k2],
            smem=1, scratch=[acc], flops=2 * length * length * 128, name=name,
        )
        return out

    q0, w0, scal, pay = call(
        functools.partial(first_body, **sizes),
        [field, field, scalars, message],
        [leaf_sizes, recv, image, start, u1, u2, v1, v2],
        smem=1, flops=small, name="first",
    )
    recv = exchange(pay)
    image = near(w0, "near1")
    q1, w1, scal, pay = call(
        functools.partial(second_body, **sizes),
        [field, field, scalars, message],
        [leaf_sizes, recv, image, q0, w0, scal, u1, u2, v1, v2],
        smem=1, flops=small, name="second",
    )
    recv = exchange(pay)
    image = near(w1, "near2")
    q2, scal, pay = call(
        functools.partial(third_body, **sizes),
        [field, scalars, shaped(num, LANES)],
        [leaf_sizes, recv, image, q0, q1, w0, w1, scal, u1, u2],
        smem=1, flops=small, name="third",
    )
    recv = exchange(pay)
    (out,) = call(
        last_body, [field], [recv, q0, q1, q2, scal, inverse], flops=small, name="last"
    )
    return out


def solution(mesh):
    in_specs = (
        P(None, AXES),
        P(None, AXES),
        P(AXES, None),
        P(AXES),
        P(),
        P(),
        P(None, None, AXES),
        P(None, None, AXES),
    )
    return jax.shard_map(
        per_device, mesh=mesh, in_specs=in_specs, out_specs=P(None, AXES), check_vma=False
    )
```

time: 462 us -> 102 us (0.22); the launches traced: 455 us -> 101 us
  blocking collectives: 282 us -> 0 us
  matrix products: 62.8 us -> 0 us
  Pallas kernels: 0 us -> 39.9 us
  other arithmetic: 28.8 us -> 0 us
  local copies, waits for them, and re-layouts: 45.1 us -> 30 us
  waiting for transfers between devices: 15 us -> 5.07 us
  starting transfers between devices: 19.5 us -> 24.6 us
    psum x7 -> x0, blocking collectives: 282 us -> none  [the longest x3 121 us: per_device(): lax.psum(jnp.sum(image * image, axis=1), ('gx', 'gy')) + epsilon]
    dot_general x13 -> x0, matrix products: 62.8 us -> none  [the longest x3 34.5 us: per_device(): nearby = jnp.dot(vector, kernel, precision=highest)]
    pallas_call x0 -> x9, Pallas kernels: none -> 39.9 us  [call(): pl.pallas_call(body, out_shape=list(outs), in_specs=specs, out_specs=[vme...]
    all_to_all x0 -> x4, starting transfers between devices: none -> 24.6 us  [exchange(): return lax.all_to_all(payload, AXES, 0, 0, tiled=True)]
    unnamed x26 -> x41, local copies, waits for them, and re-layouts: 5.7 us -> 27.5 us
    ppermute x15 -> x0, starting transfers between devices: 19.5 us -> none  [partner(): return lax.ppermute(value, axis, pairs)]
    gather x3 -> x0, local copies, waits for them, and re-layouts: 19.1 us -> none  [the longest x2 10.3 us: per_device(): start = live_mask * rhs[:, ordering]]
    ppermute x15 -> x0, waiting for transfers between devices: 15 us -> none  [partner(): return lax.ppermute(value, axis, pairs)]
  transfers between devices with their start and end apart: 15 -> 4, of which waited for: 8 -> 2; matrix products, arithmetic and copies ran while one was open for 16% -> 0% of each run, Pallas kernels for 0% -> 30%
where the time goes in v1:
time: 102 us; the launch traced here: 101 us
  Pallas kernels  39.9 us (39%)
  local copies, waits for them, and re-layouts  30 us (29%)
  starting transfers between devices  24.6 us (24%)
  waiting for transfers between devices  5.07 us (5%)
  between operations  1.45 us (1%)
    pallas_call x9, Pallas kernels, call(): pl.pallas_call(body, out_shape=list(outs), in_specs=specs, out_specs=[vme...  39.9 us
    unnamed x41, local copies, waits for them, and re-layouts  27.5 us
    all_to_all x4, starting transfers between devices, exchange(): return lax.all_to_all(payload, AXES, 0, 0, tiled=True)  24.6 us
    all_to_all x4, waiting for transfers between devices, exchange(): return lax.all_to_all(payload, AXES, 0, 0, tiled=True)  5.07 us
    all_to_all x3, local copies, waits for them, and re-layouts, exchange(): return lax.all_to_all(payload, AXES, 0, 0, tiled=True)  2.45 us
  transfers between devices with their start and end apart: 4, of which 2 were waited for; matrix products, arithmetic and copies ran while one was open for 0% of the time, Pallas kernels for 30%

profile of v1, /device:TPU:0, one launch (start us, length us, event | category | flops | bytes accessed | tf_op | source)
XLA Modules:
  0.0 101.1 jit_solution(9914280628539027762)
XLA Ops:
  0.7 0.0 copy-start.12
  0.7 1.7 %copy-done.12 = f32[5,64,2048]{2,1,0:T(8,128)S(1)} copy-done((f32[5,64,2048]{2,1,0:T(8,128)S(1)}, f32[5,64,2048]{2,1,0:T(8,128)}, u32[]{:S(2)}) %copy-start.12) | copy-done | bytes 2621464
  2.4 0.0 copy-start.13
  2.4 0.9 copy-done.13
  3.3 0.0 copy-start.14
  3.3 0.8 copy-done.14
  4.1 0.0 copy-start.15
  4.1 0.7 copy-done.15
  4.8 0.0 copy-start.17
  4.8 0.7 copy-done.17
  5.4 2.7 %start.1 = (f32[16,2048]{1,0:T(8,128)S(1)}, f32[8,2048]{1,0:T(8,128)S(1)}, f32[32,1152]{1,0:T(8,128)S(1)}, bf16[320,2048]{1,0:T(8,128)(2,1)S(1)}, bf16[320,2048]{1,0:T(8,128)(2,1)S(1)}) custom-call(s32[1]{0:T(128)S(6)} %copy.22.sizes_ref, f32[3]{0:T(128)S(1)} %copy-done.17, s32[1,2048]{1,0:T(1,128)S(1)} %copy-done.15, f32[16,2048]{1,0:T(8,128)S(1)} %copy-done.13, ...), custom_call_target="tpu_custom_call" | custom-call | flops 335544320 | bytes 5750800 | tf_op jit(solution)/shard_map/start/pallas_call | solution.py:393
  8.2 0.0 copy-start.6
  8.2 1.0 %copy-done.6 = bf16[320,2048]{1,0:T(8,128)(2,1)} copy-done((bf16[320,2048]{1,0:T(8,128)(2,1)}, bf16[320,2048]{1,0:T(8,128)(2,1)S(1)}, u32[]{:S(2)}) %copy-start.6) | copy-done | bytes 1310744
  9.2 0.0 copy-start.9
  9.2 1.1 %copy-done.9 = bf16[320,2048]{1,0:T(8,128)(2,1)} copy-done((bf16[320,2048]{1,0:T(8,128)(2,1)}, bf16[320,2048]{1,0:T(8,128)(2,1)S(1)}, u32[]{:S(2)}) %copy-start.9) | copy-done | bytes 1310744
  10.3 0.8 copy.9
  11.1 7.3 %all-to-all-start = ((f32[32,1,1152]{2,1,0:T(1,128)}), f32[32,1,1152]{2,1,0:T(1,128)S(1)}, u32[]{:S(2)}, u32[]{:S(2)}) async-start(f32[32,1,1152]{2,1,0:T(1,128)} %copy.9), calls=%async_computation | async-start | bytes 294912 | tf_op jit(solution)/shard_map/all_to_all | solution.py:406
  19.1 0.0 copy-start.18
  19.1 1.7 %copy-done.18 = f32[5,64,2048]{2,1,0:T(8,128)S(1)} copy-done((f32[5,64,2048]{2,1,0:T(8,128)S(1)}, f32[5,64,2048]{2,1,0:T(8,128)}, u32[]{:S(2)}) %copy-start.18) | copy-done | bytes 2621464
  20.8 20.8 %build.1 = (bf16[256,9216]{1,0:T(8,128)(2,1)S(1)}, bf16[256,9216]{1,0:T(8,128)(2,1)S(1)}, f32[16,2048]{1,0:T(8,128)S(1)}, bf16[320,2048]{1,0:T(8,128)(2,1)S(1)}, bf16[320,2048]{1,0:T(8,128)(2,1)S(1)}) custom-call(f32[1]{0:T(128)S(6)} %copy.23.noise_ref, f32[8,2048]{1,0:T(8,128)S(1)} %get-tuple-element.27.points_ref, ...), custom_call_target="tpu_custom_call" | custom-call | flops 2147483648 | bytes 15007748 | tf_op jit(solution)/shard_map/build/pallas_call | solution.py:393
  41.6 0.0 copy-start
  41.6 2.2 %copy-done = bf16[256,9216]{1,0:T(8,128)(2,1)} copy-done((bf16[256,9216]{1,0:T(8,128)(2,1)}, bf16[256,9216]{1,0:T(8,128)(2,1)S(1)}, u32[]{:S(2)}) %copy-start) | copy-done | bytes 4718616
  43.8 0.0 copy-start.3
  43.8 2.2 %copy-done.3 = bf16[256,9216]{1,0:T(8,128)(2,1)} copy-done((bf16[256,9216]{1,0:T(8,128)(2,1)}, bf16[256,9216]{1,0:T(8,128)(2,1)S(1)}, u32[]{:S(2)}) %copy-start.3) | copy-done | bytes 4718616
  45.9 0.0 all-to-all-done
  46.0 0.0 copy-start.7
  46.0 1.3 %copy-done.7 = bf16[320,2048]{1,0:T(8,128)(2,1)S(1)} copy-done((bf16[320,2048]{1,0:T(8,128)(2,1)S(1)}, bf16[320,2048]{1,0:T(8,128)(2,1)}, u32[]{:S(2)}) %copy-start.7) | copy-done | bytes 1310744
  47.3 0.0 copy-start.10
  47.3 1.3 %copy-done.10 = bf16[320,2048]{1,0:T(8,128)(2,1)S(1)} copy-done((bf16[320,2048]{1,0:T(8,128)(2,1)S(1)}, bf16[320,2048]{1,0:T(8,128)(2,1)}, u32[]{:S(2)}) %copy-start.10) | copy-done | bytes 1310744
  48.6 1.5 %first.1 = (f32[16,2048]{1,0:T(8,128)S(1)}, f32[16,2048]{1,0:T(8,128)S(1)}, f32[16,128]{1,0:T(8,128)S(1)}, f32[32,1152]{1,0:T(8,128)S(1)}) custom-call(s32[1]{0:T(128)S(6)} %copy.22.sizes_ref, f32[32,1152]{1,0:T(8,128)S(1)} %bitcast.21, f32[16,2048]{1,0:T(8,128)S(1)} %get-tuple-element.29.image_ref, f32[16,2048]{1,0:T(8,128)S(1)} %get-tuple-element.28.start_ref, ...), custom_call_target="tpu_custom_call" | custom-call | flops 335544320 | bytes 6070276 | tf_op jit(solution)/shard_map/first/pallas_call | solution.py:393
  50.1 0.8 copy.10
  50.9 5.8 %all-to-all-start.1 = ((f32[32,1,1152]{2,1,0:T(1,128)}), f32[32,1,1152]{2,1,0:T(1,128)S(1)}, u32[]{:S(2)}, u32[]{:S(2)}) async-start(f32[32,1,1152]{2,1,0:T(1,128)} %copy.10), calls=%async_computation.1 | async-start | bytes 294912 | tf_op jit(solution)/shard_map/all_to_all | solution.py:406
  56.8 0.0 copy-start.1
  56.8 2.3 %copy-done.1 = bf16[256,9216]{1,0:T(8,128)(2,1)S(1)} copy-done((bf16[256,9216]{1,0:T(8,128)(2,1)S(1)}, bf16[256,9216]{1,0:T(8,128)(2,1)}, u32[]{:S(2)}) %copy-start.1) | copy-done | bytes 4718616
  59.1 0.0 copy-start.4
  59.1 2.3 %copy-done.4 = bf16[256,9216]{1,0:T(8,128)(2,1)S(1)} copy-done((bf16[256,9216]{1,0:T(8,128)(2,1)S(1)}, bf16[256,9216]{1,0:T(8,128)(2,1)}, u32[]{:S(2)}) %copy-start.4) | copy-done | bytes 4718616
  61.4 3.5 %near1.1.image_ref = f32[16,2048]{1,0:T(8,128)S(1)} custom-call(f32[1]{0:T(128)S(6)} %copy.23.noise_ref, f32[16,2048]{1,0:T(8,128)S(1)} %get-tuple-element.35.vector_ref.w0_ref, bf16[256,9216]{1,0:T(8,128)(2,1)S(1)} %copy-done.1, bf16[256,9216]{1,0:T(8,128)(2,1)S(1)} %copy-done.4), custom_call_target="tpu_custom_call" | custom-call | flops 1073741824 | bytes 9699332 | tf_op jit(solution)/shard_map/near1/pallas_call | solution.py:393
  65.0 0.2 all-to-all-done.1
  65.2 0.0 copy-start.8
  65.2 1.3 %copy-done.8 = bf16[320,2048]{1,0:T(8,128)(2,1)S(1)} copy-done((bf16[320,2048]{1,0:T(8,128)(2,1)S(1)}, bf16[320,2048]{1,0:T(8,128)(2,1)}, u32[]{:S(2)}) %copy-start.8) | copy-done | bytes 1310744
  66.5 0.0 copy-start.11
  66.5 1.3 %copy-done.11 = bf16[320,2048]{1,0:T(8,128)(2,1)S(1)} copy-done((bf16[320,2048]{1,0:T(8,128)(2,1)S(1)}, bf16[320,2048]{1,0:T(8,128)(2,1)}, u32[]{:S(2)}) %copy-start.11) | copy-done | bytes 1310744
  67.8 1.5 %second.1 = (f32[16,2048]{1,0:T(8,128)S(1)}, f32[16,2048]{1,0:T(8,128)S(1)}, f32[16,128]{1,0:T(8,128)S(1)}, f32[32,1152]{1,0:T(8,128)S(1)}) custom-call(s32[1]{0:T(128)S(6)} %copy.22.sizes_ref, f32[32,1152]{1,0:T(8,128)S(1)} %bitcast.20, f32[16,2048]{1,0:T(8,128)S(1)} %near1.1.image_ref, f32[16,2048]{1,0:T(8,128)S(1)} %get-tuple-element.38.q0_ref, ...), custom_call_target="tpu_custom_call" | custom-call | flops 335544320 | bytes 6209540 | tf_op jit(solution)/shard_map/second/pallas_call | solution.py:393
  69.4 0.8 copy.11
  70.2 5.8 %all-to-all-start.2 = ((f32[32,1,1152]{2,1,0:T(1,128)}), f32[32,1,1152]{2,1,0:T(1,128)S(1)}, u32[]{:S(2)}, u32[]{:S(2)}) async-start(f32[32,1,1152]{2,1,0:T(1,128)} %copy.11), calls=%async_computation.2 | async-start | bytes 294912 | tf_op jit(solution)/shard_map/all_to_all | solution.py:406
  76.0 0.0 copy-start.2
  76.0 2.3 %copy-done.2 = bf16[256,9216]{1,0:T(8,128)(2,1)S(1)} copy-done((bf16[256,9216]{1,0:T(8,128)(2,1)S(1)}, bf16[256,9216]{1,0:T(8,128)(2,1)}, u32[]{:S(2)}) %copy-start.2) | copy-done | bytes 4718616
  78.3 0.0 copy-start.5
  78.3 2.3 %copy-done.5 = bf16[256,9216]{1,0:T(8,128)(2,1)S(1)} copy-done((bf16[256,9216]{1,0:T(8,128)(2,1)S(1)}, bf16[256,9216]{1,0:T(8,128)(2,1)}, u32[]{:S(2)}) %copy-start.5) | copy-done | bytes 4718616
  80.7 3.5 %near2.1.image_ref = f32[16,2048]{1,0:T(8,128)S(1)} custom-call(f32[1]{0:T(128)S(6)} %copy.23.noise_ref, f32[16,2048]{1,0:T(8,128)S(1)} %get-tuple-element.41.vector_ref.w1_ref, bf16[256,9216]{1,0:T(8,128)(2,1)S(1)} %copy-done.2, bf16[256,9216]{1,0:T(8,128)(2,1)S(1)} %copy-done.5), custom_call_target="tpu_custom_call" | custom-call | flops 1073741824 | bytes 9699332 | tf_op jit(solution)/shard_map/near2/pallas_call | solution.py:393
  84.2 0.0 copy-start.16
  84.2 0.0 all-to-all-done.2
  84.2 1.5 %third.1 = (f32[16,2048]{1,0:T(8,128)S(1)}, f32[16,128]{1,0:T(8,128)S(1)}, f32[32,128]{1,0:T(8,128)}) custom-call(s32[1]{0:T(128)S(6)} %copy.22.sizes_ref, f32[32,1152]{1,0:T(8,128)S(1)} %bitcast.19, f32[16,2048]{1,0:T(8,128)S(1)} %near2.1.image_ref, f32[16,2048]{1,0:T(8,128)S(1)} %get-tuple-element.38.q0_ref, f32[16,2048]{1,0:T(8,128)S(1)} %get-tuple-element.42.q1_ref, ...), custom_call_target="tpu_custom_call" | custom-call | flops 335544320 | bytes 3588100 | tf_op jit(solution)/shard_map/third/pallas_call | solution.py:393
  85.8 5.7 %all-to-all-start.3 = ((f32[32,1,128]{2,1,0:T(1,128)}), f32[32,1,128]{2,1,0:T(1,128)S(1)}, u32[]{:S(2)}, u32[]{:S(2)}) async-start(f32[32,1,128]{2,1,0:T(1,128)} %bitcast.6), calls=%async_computation.3 | async-start | bytes 32768 | tf_op jit(solution)/shard_map/all_to_all | solution.py:406
  91.4 0.0 copy-done.16
  91.4 2.3 %inverse.1.inverse_ref = s32[1,2048]{1,0:T(1,128)S(1)} custom-call(s32[1,2048]{1,0:T(1,128)S(1)} %copy-done.16), custom_call_target="tpu_custom_call" | custom-call | flops 536870912 | bytes 16384 | tf_op jit(solution)/shard_map/inverse/pallas_call | solution.py:393
  93.7 4.8 %all-to-all-done.3 = f32[32,1,128]{2,1,0:T(1,128)S(1)} async-done(((f32[32,1,128]{2,1,0:T(1,128)}), f32[32,1,128]{2,1,0:T(1,128)S(1)}, u32[]{:S(2)}, u32[]{:S(2)}) %all-to-all-start.3) | async-done | bytes 16416 | tf_op jit(solution)/shard_map/all_to_all | solution.py:406
  98.5 2.6 %last.1 = f32[16,2048]{1,0:T(8,128)} custom-call(f32[32,128]{1,0:T(8,128)S(1)} %bitcast.25, f32[16,2048]{1,0:T(8,128)S(1)} %get-tuple-element.38.q0_ref, f32[16,2048]{1,0:T(8,128)S(1)} %get-tuple-element.42.q1_ref, f32[16,2048]{1,0:T(8,128)S(1)} %get-tuple-element.45.q2_ref, f32[16,128]{1,0:T(8,128)S(1)} %get-tuple-element.46.old_ref, ...), custom_call_target="tpu_custom_call" | custom-call | flops 335544320 | bytes 557056 | tf_op jit(solution)/shard_map/last/pallas_call | solution.py:393
  (3 shorter events, 0.0 us)
Async XLA Ops:
  0.7 1.7 %copy-start.12 = (f32[5,64,2048]{2,1,0:T(8,128)S(1)}, f32[5,64,2048]{2,1,0:T(8,128)}, u32[]{:S(2)}) copy-start(f32[5,64,2048]{2,1,0:T(8,128)} %param.15) | copy-start | bytes 7864324
  2.4 0.9 copy-start.13
  3.3 0.8 copy-start.14
  4.1 0.7 copy-start.15
  4.8 0.7 copy-start.17
  8.2 1.0 %copy-start.6 = (bf16[320,2048]{1,0:T(8,128)(2,1)}, bf16[320,2048]{1,0:T(8,128)(2,1)S(1)}, u32[]{:S(2)}) copy-start(bf16[320,2048]{1,0:T(8,128)(2,1)S(1)} %get-tuple-element.32.v1_ref) | copy-start | bytes 3932164
  9.2 1.1 %copy-start.9 = (bf16[320,2048]{1,0:T(8,128)(2,1)}, bf16[320,2048]{1,0:T(8,128)(2,1)S(1)}, u32[]{:S(2)}) copy-start(bf16[320,2048]{1,0:T(8,128)(2,1)S(1)} %get-tuple-element.33.v2_ref) | copy-start | bytes 3932164
  11.1 34.9 %all-to-all-start = ((f32[32,1,1152]{2,1,0:T(1,128)}), f32[32,1,1152]{2,1,0:T(1,128)S(1)}, u32[]{:S(2)}, u32[]{:S(2)}) async-start(f32[32,1,1152]{2,1,0:T(1,128)} %copy.9), calls=%async_computation | async-start | bytes 294912 | tf_op jit(solution)/shard_map/all_to_all | solution.py:406
  19.1 1.7 %copy-start.18 = (f32[5,64,2048]{2,1,0:T(8,128)S(1)}, f32[5,64,2048]{2,1,0:T(8,128)}, u32[]{:S(2)}) copy-start(f32[5,64,2048]{2,1,0:T(8,128)} %param.14) | copy-start | bytes 7864324
  41.6 2.2 %copy-start = (bf16[256,9216]{1,0:T(8,128)(2,1)}, bf16[256,9216]{1,0:T(8,128)(2,1)S(1)}, u32[]{:S(2)}) copy-start(bf16[256,9216]{1,0:T(8,128)(2,1)S(1)} %get-tuple-element.36.high_ref) | copy-start | bytes 14155780
  43.8 2.2 %copy-start.3 = (bf16[256,9216]{1,0:T(8,128)(2,1)}, bf16[256,9216]{1,0:T(8,128)(2,1)S(1)}, u32[]{:S(2)}) copy-start(bf16[256,9216]{1,0:T(8,128)(2,1)S(1)} %get-tuple-element.37.low_ref) | copy-start | bytes 14155780
  46.0 1.3 %copy-start.7 = (bf16[320,2048]{1,0:T(8,128)(2,1)S(1)}, bf16[320,2048]{1,0:T(8,128)(2,1)}, u32[]{:S(2)}) copy-start(bf16[320,2048]{1,0:T(8,128)(2,1)} %copy-done.6) | copy-start | bytes 3932164
  47.3 1.3 %copy-start.10 = (bf16[320,2048]{1,0:T(8,128)(2,1)S(1)}, bf16[320,2048]{1,0:T(8,128)(2,1)}, u32[]{:S(2)}) copy-start(bf16[320,2048]{1,0:T(8,128)(2,1)} %copy-done.9) | copy-start | bytes 3932164
  50.9 14.3 %all-to-all-start.1 = ((f32[32,1,1152]{2,1,0:T(1,128)}), f32[32,1,1152]{2,1,0:T(1,128)S(1)}, u32[]{:S(2)}, u32[]{:S(2)}) async-start(f32[32,1,1152]{2,1,0:T(1,128)} %copy.10), calls=%async_computation.1 | async-start | bytes 294912 | tf_op jit(solution)/shard_map/all_to_all | solution.py:406
  56.8 2.3 %copy-start.1 = (bf16[256,9216]{1,0:T(8,128)(2,1)S(1)}, bf16[256,9216]{1,0:T(8,128)(2,1)}, u32[]{:S(2)}) copy-start(bf16[256,9216]{1,0:T(8,128)(2,1)} %copy-done) | copy-start | bytes 14155780
  59.1 2.3 %copy-start.4 = (bf16[256,9216]{1,0:T(8,128)(2,1)S(1)}, bf16[256,9216]{1,0:T(8,128)(2,1)}, u32[]{:S(2)}) copy-start(bf16[256,9216]{1,0:T(8,128)(2,1)} %copy-done.3) | copy-start | bytes 14155780
  65.2 1.3 %copy-start.8 = (bf16[320,2048]{1,0:T(8,128)(2,1)S(1)}, bf16[320,2048]{1,0:T(8,128)(2,1)}, u32[]{:S(2)}) copy-start(bf16[320,2048]{1,0:T(8,128)(2,1)} %copy-done.6) | copy-start | bytes 3932164
  66.5 1.3 %copy-start.11 = (bf16[320,2048]{1,0:T(8,128)(2,1)S(1)}, bf16[320,2048]{1,0:T(8,128)(2,1)}, u32[]{:S(2)}) copy-start(bf16[320,2048]{1,0:T(8,128)(2,1)} %copy-done.9) | copy-start | bytes 3932164
  70.2 14.1 %all-to-all-start.2 = ((f32[32,1,1152]{2,1,0:T(1,128)}), f32[32,1,1152]{2,1,0:T(1,128)S(1)}, u32[]{:S(2)}, u32[]{:S(2)}) async-start(f32[32,1,1152]{2,1,0:T(1,128)} %copy.11), calls=%async_computation.2 | async-start | bytes 294912 | tf_op jit(solution)/shard_map/all_to_all | solution.py:406
  76.0 2.3 %copy-start.2 = (bf16[256,9216]{1,0:T(8,128)(2,1)S(1)}, bf16[256,9216]{1,0:T(8,128)(2,1)}, u32[]{:S(2)}) copy-start(bf16[256,9216]{1,0:T(8,128)(2,1)} %copy-done) | copy-start | bytes 14155780
  78.3 2.3 %copy-start.5 = (bf16[256,9216]{1,0:T(8,128)(2,1)S(1)}, bf16[256,9216]{1,0:T(8,128)(2,1)}, u32[]{:S(2)}) copy-start(bf16[256,9216]{1,0:T(8,128)(2,1)} %copy-done.3) | copy-start | bytes 14155780
  84.2 7.2 %copy-start.16 = (s32[1,2048]{1,0:T(1,128)S(1)}, s32[1,2048]{1,0:T(1,128)}, u32[]{:S(2)}) copy-start(s32[1,2048]{1,0:T(1,128)} %order_ref.3) | copy-start | bytes 24580
  85.8 12.8 %all-to-all-start.3 = ((f32[32,1,128]{2,1,0:T(1,128)}), f32[32,1,128]{2,1,0:T(1,128)S(1)}, u32[]{:S(2)}, u32[]{:S(2)}) async-start(f32[32,1,128]{2,1,0:T(1,128)} %bitcast.6), calls=%async_computation.3 | async-start | bytes 32768 | tf_op jit(solution)/shard_map/all_to_all | solution.py:406

commit v2 on v1

--- a/solution.py
+++ b/solution.py
@@ -97,8 +97,8 @@
             start = lev * rank + block * group
             piece = jnp.where(mask, both[start : start + group], 0.0)
             rows = jnp.where(level == lev, jnp.sum(piece, axis=0, keepdims=True), rows)
-        pay_ref[:, block * LANES : (block + 1) * LANES] = rows
-    pay_ref[:, rank * vectors :] = jnp.broadcast_to(dots, (num, LANES))
+        pay_ref[:, 0, block * LANES : (block + 1) * LANES] = rows
+    pay_ref[:, 0, rank * vectors :] = jnp.broadcast_to(dots, (num, LANES))
 
 
 def receive_coefs(recv_ref, vectors, levels, rank):
@@ -109,7 +109,7 @@
     pieces = []
     for lev in range(levels):
         for block in range(rank // group):
-            part = recv_ref[:, block * LANES : (block + 1) * LANES]
+            part = recv_ref[:, 0, block * LANES : (block + 1) * LANES]
             total = jnp.sum(jnp.where(level == lev, part, 0.0), axis=0, keepdims=True)
             pieces.append(jnp.where(mask, jnp.broadcast_to(total, mask.shape), 0.0))
     flipped = jnp.concatenate(pieces, axis=0).T
@@ -138,12 +138,23 @@
 
 
 def start_body(
-    sizes_ref, scales_ref, order_ref, rhs_ref, coords_ref, v_ref,
-    start_ref, points_ref, pay_ref, v1_ref, v2_ref, pad_ref, *, levels, rank,
-):
+    sizes_ref, scales_ref, order_hbm, rhs_hbm, coords_hbm, v_hbm,
+    start_ref, points_ref, pay_ref, v1_hbm, v2_hbm,
+    order_ref, rhs_ref, coords_ref, pad_ref, v_ref, v1_ref, v2_ref, sem, *, levels, rank,
+):
+    loads = [
+        pltpu.make_async_copy(source, target, sem.at[n])
+        for n, (source, target) in enumerate(
+            [(order_hbm, order_ref), (rhs_hbm, rhs_ref), (coords_hbm, coords_ref), (v_hbm, v_ref)]
+        )
+    ]
+    for load in loads:
+        load.start()
     vectors, length = rhs_ref.shape
     dims = coords_ref.shape[0]
     pad_ref[...] = jnp.zeros(pad_ref.shape, f32)
+    for load in loads[:3]:
+        load.wait()
     pad_ref[:dims, :] = coords_ref[...]
     stacked = jnp.concatenate(
         [p.astype(f32) for p in split(rhs_ref[...], 3)]
@@ -163,81 +174,127 @@
         rest = chosen[3 * vectors :]
         value = rest[:rows] + rest[rows : 2 * rows] + rest[2 * rows :]
         points_ref[:, base : base + TILE] = value * scale
+    loads[3].wait()
     high, low = split(v_ref[...], 2)
     v1_ref[...] = high
     v2_ref[...] = low
+    stores = [
+        pltpu.make_async_copy(v1_ref, v1_hbm, sem.at[4]),
+        pltpu.make_async_copy(v2_ref, v2_hbm, sem.at[5]),
+    ]
+    for store in stores:
+        store.start()
     start = start_ref[...]
     dots = pack_dots([(start, start)], vectors)
     send_coefs(start, high, low, pay_ref, dots, levels, rank)
-
-
-def dense(vector, high_ref, low_ref, acc_ref):
-    vectors, length = vector.shape
-    stacked = jnp.concatenate(split(vector, 3), axis=0)
+    for store in stores:
+        store.wait()
+
+
+def add_panel(stacked, high_ref, low_ref, acc_ref, base, offset):
+    width = acc_ref.shape[1] - base
+    own = stacked[:, base : base + TILE]
+    for half in (high_ref, low_ref):
+        acc_ref[:, base:] += dot(own, half[:, offset : offset + width])
+        if width > TILE:
+            acc_ref[:, base : base + TILE] += dot_nt(
+                stacked[:, base + TILE :], half[:, offset + TILE : offset + width]
+            )
+
+
+def finish(acc_ref, noise_ref, vector):
+    vectors = vector.shape[0]
+    out = acc_ref[...]
+    out = out[:vectors] + out[vectors : 2 * vectors] + out[2 * vectors :]
+    return LN2 * out + noise_ref[0] * vector
+
+
+def panels(length):
     offset = 0
     for base in range(0, length, TILE):
-        width = length - base
-        own = stacked[:, base : base + TILE]
-        high = high_ref[:, offset : offset + width]
-        low = low_ref[:, offset : offset + width]
-        part = dot(own, high) + dot(own, low)
-        if base == 0:
-            acc_ref[...] = part
-        else:
-            acc_ref[:, base:] += part
-        if width > TILE:
-            rest = stacked[:, base + TILE :]
-            acc_ref[:, base : base + TILE] += dot_nt(rest, high[:, TILE:]) + dot_nt(
-                rest, low[:, TILE:]
-            )
-        offset += width
-    out = acc_ref[...]
-    return out[:vectors] + out[vectors : 2 * vectors] + out[2 * vectors :]
+        yield base, offset, length - base
+        offset += length - base
 
 
 def build_body(
-    noise_ref, points_ref, start_ref, u_ref, high_ref, low_ref, image_ref, u1_ref, u2_ref,
-    column_ref, acc_ref, *, dims,
+    noise_ref, points_ref, start_ref, u_hbm, high_hbm, low_hbm, image_ref, u1_ref, u2_ref,
+    u_ref, wide_ref, high_ref, low_ref, acc_ref, sem, *, dims,
 ):
     length = points_ref.shape[1]
     step = 16
-    column_ref[...] = points_ref[...].T
+    load = pltpu.make_async_copy(u_hbm, u_ref, sem.at[0])
+    load.start()
+    columns = points_ref[...].T
+    for dim in range(dims):
+        wide_ref[dim] = jnp.broadcast_to(columns[:, dim : dim + 1], (length, LANES))
+    start = start_ref[...]
+    stacked = jnp.concatenate(split(start, 3), axis=0)
+    acc_ref[...] = jnp.zeros(acc_ref.shape, f32)
+    copies = []
+    for base, offset, width in panels(length):
+        for row in range(0, TILE, step):
+            column = [wide_ref[dim, base + row : base + row + step, :] for dim in range(dims)]
+            for lane in range(base, length, LANES):
+                square = None
+                for dim in range(dims):
+                    differ = column[dim] - points_ref[dim : dim + 1, lane : lane + LANES]
+                    square = differ * differ if square is None else square + differ * differ
+                square = jnp.maximum(square, 1e-30)
+                distance = square * lax.rsqrt(square)
+                value = (1.0 / LN2 + distance) * jnp.exp2(-distance)
+                high, low = split(value, 2)
+                place = offset + lane - base
+                high_ref[row : row + step, place : place + LANES] = high
+                low_ref[row : row + step, place : place + LANES] = low
+        for source, target in ((high_ref, high_hbm), (low_ref, low_hbm)):
+            copy = pltpu.make_async_copy(
+                source.at[:, offset : offset + width],
+                target.at[:, offset : offset + width],
+                sem.at[1 + len(copies)],
+            )
+            copy.start()
+            copies.append(copy)
+        add_panel(stacked, high_ref, low_ref, acc_ref, base, offset)
+    image_ref[...] = finish(acc_ref, noise_ref, start)
+    load.wait()
     high, low = split(u_ref[...], 2)
     u1_ref[...] = high
     u2_ref[...] = low
-    offset = 0
-    for base in range(0, length, TILE):
-        width = length - base
-
-        def rows_step(index, carry, base=base, width=width, offset=offset):
-            row = pl.multiple_of(index * step, step)
-            square = None
-            for dim in range(dims):
-                differ = (
-                    column_ref[pl.ds(base + row, step), dim : dim + 1]
-                    - points_ref[dim : dim + 1, base:]
-                )
-                square = differ * differ if square is None else square + differ * differ
-            square = jnp.maximum(square, 1e-30)
-            distance = square * lax.rsqrt(square)
-            value = (1.0 + LN2 * distance) * jnp.exp2(-distance)
-            high, low = split(value, 2)
-            high_ref[pl.ds(row, step), offset : offset + width] = high
-            low_ref[pl.ds(row, step), offset : offset + width] = low
-            return carry
-
-        lax.fori_loop(0, TILE // step, rows_step, 0)
-        offset += width
-    start = start_ref[...]
-    image_ref[...] = dense(start, high_ref, low_ref, acc_ref) + noise_ref[0] * start
-
-
-def dense_body(noise_ref, vector_ref, high_ref, low_ref, image_ref, acc_ref):
+    for copy in copies:
+        copy.wait()
+
+
+def near_body(
+    noise_ref, vector_ref, high_hbm, low_hbm, *refs, order
+):
+    if order:
+        order_ref, image_ref, inverse_ref, high_ref, low_ref, acc_ref, sem = refs
+    else:
+        image_ref, high_ref, low_ref, acc_ref, sem = refs
     vector = vector_ref[...]
-    image_ref[...] = dense(vector, high_ref, low_ref, acc_ref) + noise_ref[0] * vector
-
-
-def inverse_body(order_ref, inverse_ref):
+    length = vector.shape[1]
+    copies = []
+    for base, offset, width in panels(length):
+        for source, target in ((high_hbm, high_ref), (low_hbm, low_ref)):
+            copy = pltpu.make_async_copy(
+                source.at[:, offset : offset + width],
+                target.at[:, offset : offset + width],
+                sem.at[len(copies)],
+            )
+            copy.start()
+            copies.append(copy)
+    stacked = jnp.concatenate(split(vector, 3), axis=0)
+    acc_ref[...] = jnp.zeros(acc_ref.shape, f32)
+    if order:
+        inverse_ref[...] = inverse_of(order_ref)
+    for number, (base, offset, width) in enumerate(panels(length)):
+        copies[2 * number].wait()
+        copies[2 * number + 1].wait()
+        add_panel(stacked, high_ref, low_ref, acc_ref, base, offset)
+    image_ref[...] = finish(acc_ref, noise_ref, vector)
+
+
+def inverse_of(order_ref):
     length = order_ref.shape[1]
     place = lax.broadcasted_iota(jnp.int32, (8, TILE), 1).astype(f32)
     row_id = lax.broadcasted_iota(jnp.int32, (8, TILE), 0)
@@ -246,16 +303,27 @@
         weights = jnp.where(row_id == 0, place, float(base // TILE))
         hot = one_hot(order_ref[:, base : base + TILE], length)
         total = total + dot_nt(weights.astype(bf16), hot)
-    inverse_ref[...] = (total[0:1] + total[1:2] * float(TILE)).astype(jnp.int32)
+    return (total[0:1] + total[1:2] * float(TILE)).astype(jnp.int32)
+
+
+def load_pair(high_hbm, low_hbm, high_ref, low_ref, sem):
+    loads = [
+        pltpu.make_async_copy(high_hbm, high_ref, sem.at[0]),
+        pltpu.make_async_copy(low_hbm, low_ref, sem.at[1]),
+    ]
+    for load in loads:
+        load.start()
+    return loads
 
 
 def first_body(
-    sizes_ref, recv_ref, image_ref, start_ref, u1_ref, u2_ref, v1_ref, v2_ref,
-    q0_ref, w0_ref, scal_ref, pay_ref, *, levels, rank,
-):
+    sizes_ref, recv_ref, image_ref, start_ref, u1_ref, u2_ref, v1_hbm, v2_hbm,
+    q0_ref, w0_ref, scal_ref, pay_ref, v1_ref, v2_ref, sem, *, levels, rank,
+):
+    loads = load_pair(v1_hbm, v2_hbm, v1_ref, v2_ref, sem)
     vectors, length = start_ref.shape
     live = live_row(sizes_ref[0], length)
-    (norm,) = unpack_dots(recv_ref[:, rank * vectors :], 1, vectors)
+    (norm,) = unpack_dots(recv_ref[:, 0, rank * vectors :], 1, vectors)
     beta = jnp.sqrt(norm + EPSILON)
     inverse = 1.0 / beta
     distant = expand(receive_coefs(recv_ref, vectors, levels, rank), u1_ref[...], u2_ref[...])
@@ -265,6 +333,8 @@
     w0_ref[...] = w0
     scal_ref[...] = jnp.broadcast_to(beta, scal_ref.shape)
     dots = pack_dots([(q0, q0), (q0, w0), (w0, w0)], vectors)
+    for load in loads:
+        load.wait()
     send_coefs(w0, v1_ref[...], v2_ref[...], pay_ref, dots, levels, rank)
 
 
@@ -281,13 +351,14 @@
 
 
 def second_body(
-    sizes_ref, recv_ref, image_ref, q0_ref, w0_ref, old_ref, u1_ref, u2_ref, v1_ref, v2_ref,
-    q1_ref, w1_ref, scal_ref, pay_ref, *, levels, rank,
-):
+    sizes_ref, recv_ref, image_ref, q0_ref, w0_ref, old_ref, u1_ref, u2_ref, v1_hbm, v2_hbm,
+    q1_ref, w1_ref, scal_ref, pay_ref, v1_ref, v2_ref, sem, *, levels, rank,
+):
+    loads = load_pair(v1_hbm, v2_hbm, v1_ref, v2_ref, sem)
     vectors, length = q0_ref.shape
     live = live_row(sizes_ref[0], length)
     (beta,) = get_scalars(old_ref, 1)
-    g00, h00, norm = unpack_dots(recv_ref[:, rank * vectors :], 3, vectors)
+    g00, h00, norm = unpack_dots(recv_ref[:, 0, rank * vectors :], 3, vectors)
     rest = norm - 2.0 * h00 * h00 + h00 * h00 * g00
     h10 = jnp.sqrt(jnp.maximum(rest, 0.0) + EPSILON)
     inverse = 1.0 / h10
@@ -300,6 +371,8 @@
     q1_ref[...] = q1
     w1_ref[...] = w1
     dots = pack_dots([(q0, w1), (q1, w1), (w1, w1), (q0, q1), (q1, q1)], vectors)
+    for load in loads:
+        load.wait()
     send_coefs(w1, v1_ref[...], v2_ref[...], pay_ref, dots, levels, rank)
 
 
@@ -310,7 +383,7 @@
     vectors, length = q0_ref.shape
     live = live_row(sizes_ref[0], length)
     beta, g00, h00, h10 = get_scalars(old_ref, 4)
-    h01, h11, norm, g01, g11 = unpack_dots(recv_ref[:, rank * vectors :], 5, vectors)
+    h01, h11, norm, g01, g11 = unpack_dots(recv_ref[:, 0, rank * vectors :], 5, vectors)
     rest = (
         norm - 2.0 * (h01 * h01 + h11 * h11)
         + (h01 * h01 * g00 + h11 * h11 * g11 + 2.0 * h01 * h11 * g01)
@@ -330,7 +403,8 @@
     dots = pack_dots(
         [(q0, w2), (q1, w2), (q2, w2), (w2, w2), (q0, q2), (q1, q2), (q2, q2)], vectors
     )
-    pay_ref[...] = jnp.broadcast_to(dots, pay_ref.shape)
+    num, _, width = pay_ref.shape
+    pay_ref[:, 0, :] = jnp.broadcast_to(dots, (num, width))
 
 
 def least_squares(columns, beta):
@@ -368,7 +442,7 @@
 def last_body(recv_ref, q0_ref, q1_ref, q2_ref, old_ref, inverse_ref, out_ref):
     vectors, length = q0_ref.shape
     beta, g00, h00, h10, g01, g11, h01, h11, h21 = get_scalars(old_ref, 9)
-    h02, h12, h22, norm, g02, g12, g22 = unpack_dots(recv_ref[...], 7, vectors)
+    h02, h12, h22, norm, g02, g12, g22 = unpack_dots(recv_ref[:, 0, :], 7, vectors)
     rest = (
         norm - 2.0 * (h02 * h02 + h12 * h12 + h22 * h22)
         + (h02 * h02 * g00 + h12 * h12 * g11 + h22 * h22 * g22)
@@ -385,21 +459,19 @@
         )
 
 
-def call(body, outs, args, smem=0, scratch=(), flops=0, limit=20, name=None):
-    smem_spec = pl.BlockSpec(memory_space=pltpu.SMEM)
-    vmem_spec = pl.BlockSpec(memory_space=pltpu.VMEM)
-    specs = [smem_spec] * smem + [vmem_spec] * (len(args) - smem)
-    total = sum(math.prod(a.shape) * a.dtype.itemsize for a in list(args) + list(outs))
+def call(body, outs, args, scratch=(), flops=0, limit=20000, name=None):
+    spaces = dict(s=pltpu.SMEM, v=pltpu.VMEM, h=pltpu.HBM)
+    total = sum(math.prod(a.shape) * a.dtype.itemsize for _, a in list(args) + list(outs))
     return pl.pallas_call(
         body,
-        out_shape=list(outs),
-        in_specs=specs,
-        out_specs=[vmem_spec] * len(outs),
+        out_shape=[pltpu.HBM(a.shape, a.dtype) if m == "h" else a for m, a in outs],
+        in_specs=[pl.BlockSpec(memory_space=spaces[m]) for m, _ in args],
+        out_specs=[pl.BlockSpec(memory_space=spaces[m]) for m, _ in outs],
         scratch_shapes=list(scratch),
-        compiler_params=pltpu.CompilerParams(vmem_limit_bytes=limit * 1024 * 1024),
+        compiler_params=pltpu.CompilerParams(vmem_limit_bytes=limit * 1024),
         cost_estimate=pl.CostEstimate(flops=flops, bytes_accessed=total, transcendentals=0),
         name=name,
-    )(*args)
+    )(*[pltpu.with_memory_space_constraint(a, pltpu.HBM) if m == "h" else a for m, a in args])
 
 
 def exchange(payload):
@@ -422,65 +494,91 @@
     def shaped(*shape, dtype=f32):
         return jax.ShapeDtypeStruct(shape, dtype)
 
-    field = shaped(vectors, length)
+    field = ("v", shaped(vectors, length))
     factor = shaped(levels * rank, length, dtype=bf16)
-    scalars = shaped(vectors, LANES)
-    message = shaped(num, rank * vectors + LANES)
+    scalars = ("v", shaped(vectors, LANES))
+    message = ("v", shaped(num, 1, rank * vectors + LANES))
+    panel = shaped(TILE, packed, dtype=bf16)
     acc = pltpu.VMEM((3 * vectors, length), f32)
+    panel_space = pltpu.VMEM((TILE, packed), bf16)
+    factor_space = pltpu.VMEM((levels * rank, length), bf16)
+    whole_space = pltpu.VMEM((levels * rank, length), f32)
     sizes = dict(levels=levels, rank=rank)
     small = 2 * levels * rank * length * 256
 
+    def arrays(memory, *values):
+        return [(memory, value) for value in values]
+
     start, points, pay, v1, v2 = call(
         functools.partial(start_body, **sizes),
-        [field, shaped(padded, length), message, factor, factor],
-        [leaf_sizes, inverse_scales, leaf_order, rhs, coordinates, v_flat],
-        smem=2, scratch=[pltpu.VMEM((padded, length), f32)], flops=small, name="start",
+        [field, ("v", shaped(padded, length)), message, ("h", factor), ("h", factor)],
+        arrays("s", leaf_sizes, inverse_scales)
+        + arrays("h", leaf_order, rhs, coordinates, v_flat),
+        scratch=[
+            pltpu.VMEM((1, length), jnp.int32),
+            pltpu.VMEM((vectors, length), f32),
+            pltpu.VMEM((dims, length), f32),
+            pltpu.VMEM((padded, length), f32),
+            whole_space,
+            factor_space,
+            factor_space,
+            pltpu.SemaphoreType.DMA((6,)),
+        ],
+        flops=small, name="start",
     )
     recv = exchange(pay)
     k1, k2, image, u1, u2 = call(
         functools.partial(build_body, dims=dims),
-        [shaped(TILE, packed, dtype=bf16)] * 2 + [field, factor, factor],
-        [noise_var, points, start, u_flat],
-        smem=1, scratch=[pltpu.VMEM((length, padded), f32), acc],
-        flops=2 * length * length * 256, limit=30, name="build",
-    )
-    (inverse,) = call(
-        inverse_body, [shaped(1, length, dtype=jnp.int32)], [leaf_order],
-        flops=2 * length * length * 64, name="inverse",
-    )
-
-    def near(vector, name):
-        (out,) = call(
-            dense_body, [field], [noise_var, vector, k1, k2],
-            smem=1, scratch=[acc], flops=2 * length * length * 128, name=name,
+        [("h", panel), ("h", panel), field, ("v", factor), ("v", factor)],
+        arrays("s", noise_var) + arrays("v", points, start) + arrays("h", u_flat),
+        scratch=[
+            whole_space,
+            pltpu.VMEM((dims, length, LANES), f32),
+            panel_space,
+            panel_space,
+            acc,
+            pltpu.SemaphoreType.DMA((1 + 2 * blocks,)),
+        ],
+        flops=2 * length * length * 256, limit=40000, name="build",
+    )
+
+    def near(vector, name, order):
+        return call(
+            functools.partial(near_body, order=order),
+            [field] + ([("v", shaped(1, length, dtype=jnp.int32))] if order else []),
+            arrays("s", noise_var) + arrays("v", vector) + arrays("h", k1, k2)
+            + (arrays("v", leaf_order) if order else []),
+            scratch=[panel_space, panel_space, acc, pltpu.SemaphoreType.DMA((2 * blocks,))],
+            flops=2 * length * length * 128, limit=30000, name=name,
         )
-        return out
-
+
+    pair_space = [factor_space, factor_space, pltpu.SemaphoreType.DMA((2,))]
     q0, w0, scal, pay = call(
         functools.partial(first_body, **sizes),
         [field, field, scalars, message],
-        [leaf_sizes, recv, image, start, u1, u2, v1, v2],
-        smem=1, flops=small, name="first",
+        arrays("s", leaf_sizes) + arrays("v", recv, image, start, u1, u2) + arrays("h", v1, v2),
+        scratch=pair_space, flops=small, name="first",
     )
     recv = exchange(pay)
-    image = near(w0, "near1")
+    (image,) = near(w0, "near1", False)
     q1, w1, scal, pay = call(
         functools.partial(second_body, **sizes),
         [field, field, scalars, message],
-        [leaf_sizes, recv, image, q0, w0, scal, u1, u2, v1, v2],
-        smem=1, flops=small, name="second",
+        arrays("s", leaf_sizes) + arrays("v", recv, image, q0, w0, scal, u1, u2)
+        + arrays("h", v1, v2),
+        scratch=pair_space, flops=small, name="second",
     )
     recv = exchange(pay)
-    image = near(w1, "near2")
+    image, inverse = near(w1, "near2", True)
     q2, scal, pay = call(
         functools.partial(third_body, **sizes),
-        [field, scalars, shaped(num, LANES)],
-        [leaf_sizes, recv, image, q0, q1, w0, w1, scal, u1, u2],
-        smem=1, flops=small, name="third",
+        [field, scalars, ("v", shaped(num, 1, LANES))],
+        arrays("s", leaf_sizes) + arrays("v", recv, image, q0, q1, w0, w1, scal, u1, u2),
+        flops=small, name="third",
     )
     recv = exchange(pay)
     (out,) = call(
-        last_body, [field], [recv, q0, q1, q2, scal, inverse], flops=small, name="last"
+        last_body, [field], arrays("v", recv, q0, q1, q2, scal, inverse), flops=small, name="last"
     )
     return out
 

time: 102 us -> 77.5 us (0.76)
  local copies, waits for them, and re-layouts: 30 us -> 0.65 us
  blocking collectives: 0 us -> 12.8 us
  starting transfers between devices: 24.6 us -> 18.7 us
  waiting for transfers between devices: 5.07 us -> 0.35 us
  Pallas kernels: 39.9 us -> 43.2 us
    unnamed x41 -> x4, local copies, waits for them, and re-layouts: 27.5 us -> 0.65 us
    all_to_all x0 -> x1, blocking collectives: none -> 12.8 us  [exchange(): return lax.all_to_all(payload, AXES, 0, 0, tiled=True)]
    all_to_all x4 -> x3, starting transfers between devices: 24.6 us -> 18.7 us  [exchange(): return lax.all_to_all(payload, AXES, 0, 0, tiled=True)]
    all_to_all x4 -> x3, waiting for transfers between devices: 5.07 us -> 0.35 us  [exchange(): return lax.all_to_all(payload, AXES, 0, 0, tiled=True)]
    pallas_call x9 -> x8, Pallas kernels: 39.9 us -> 43.2 us  [call(): pl.pallas_call(body, out_shape=[pltpu.HBM(a.shape, a.dtype) if m == 'h' e...]
    all_to_all x3 -> x0, local copies, waits for them, and re-layouts: 2.45 us -> none  [exchange(): return lax.all_to_all(payload, AXES, 0, 0, tiled=True)]
  transfers between devices with their start and end apart: 4 -> 3, of which waited for: 2 -> 1; matrix products, arithmetic and copies ran while one was open for 0% -> 0% of each run, Pallas kernels for 30% -> 34%
where the time goes in v2:
time: 77.5 us; the launch traced here: 77.1 us
  Pallas kernels  43.2 us (56%)
  starting transfers between devices  18.7 us (24%)
  blocking collectives  12.8 us (17%)
  between operations  1.41 us (2%)
    pallas_call x8, Pallas kernels, call(): pl.pallas_call(body, out_shape=[pltpu.HBM(a.shape, a.dtype) if m == 'h' e...  43.2 us
    all_to_all x3, starting transfers between devices, exchange(): return lax.all_to_all(payload, AXES, 0, 0, tiled=True)  18.7 us
    all_to_all x1, blocking collectives, exchange(): return lax.all_to_all(payload, AXES, 0, 0, tiled=True)  12.8 us
  transfers between devices with their start and end apart: 3, of which 1 were waited for; matrix products, arithmetic and copies ran while one was open for 0% of the time, Pallas kernels for 34%

profile of v2, /device:TPU:0, one launch (start us, length us, event | category | flops | bytes accessed | tf_op | source)
XLA Modules:
  0.0 77.1 jit_solution(154231981625845174)
XLA Ops:
  0.7 0.0 copy-start.1
  0.7 0.6 copy-done.1
  1.3 5.7 %start.1 = (f32[16,2048]{1,0:T(8,128)S(1)}, f32[8,2048]{1,0:T(8,128)S(1)}, f32[32,1,1152]{2,1,0:T(1,128)}, bf16[320,2048]{1,0:T(8,128)(2,1)}, bf16[320,2048]{1,0:T(8,128)(2,1)}) custom-call(s32[1]{0:T(128)S(6)} %copy.9.sizes_ref, f32[3]{0:T(128)S(1)} %copy-done.1, s32[1,2048]{1,0:T(1,128)} %refs_0_.1, f32[16,2048]{1,0:T(8,128)} %rhs_hbm.1, ...), custom_call_target="tpu_custom_call" | custom-call | flops 335544320 | bytes 5750800 | tf_op jit(solution)/shard_map/start/pallas_call | solution.py:465
  7.0 7.5 %all-to-all-start = ((f32[32,1,1152]{2,1,0:T(1,128)}), f32[32,1,1152]{2,1,0:T(1,128)S(1)}, u32[]{:S(2)}, u32[]{:S(2)}) async-start(f32[32,1,1152]{2,1,0:T(1,128)} %get-tuple-element.28), calls=%async_computation | async-start | bytes 294912 | tf_op jit(solution)/shard_map/all_to_all | solution.py:478
  15.2 9.6 %build.1 = (bf16[256,9216]{1,0:T(8,128)(2,1)}, bf16[256,9216]{1,0:T(8,128)(2,1)}, f32[16,2048]{1,0:T(8,128)S(1)}, bf16[320,2048]{1,0:T(8,128)(2,1)S(1)}, bf16[320,2048]{1,0:T(8,128)(2,1)S(1)}) custom-call(f32[1]{0:T(128)S(6)} %copy.10.noise_ref, f32[8,2048]{1,0:T(8,128)S(1)} %get-tuple-element.29.points_ref, f32[16,2048]{1,0:T(8,128)S(1)} %get-tuple-element.30.start_ref, ...), custom_call_target="tpu_custom_call" | custom-call | flops 2147483648 | bytes 15007748 | tf_op jit(solution)/shard_map/build/pallas_call | solution.py:465
  24.8 0.0 all-to-all-done.recv_ref
  24.8 4.1 %first.1 = (f32[16,2048]{1,0:T(8,128)S(1)}, f32[16,2048]{1,0:T(8,128)S(1)}, f32[16,128]{1,0:T(8,128)S(1)}, f32[32,1,1152]{2,1,0:T(1,128)}) custom-call(s32[1]{0:T(128)S(6)} %copy.9.sizes_ref, f32[32,1,1152]{2,1,0:T(1,128)S(1)} %all-to-all-done.recv_ref, f32[16,2048]{1,0:T(8,128)S(1)} %get-tuple-element.31.image_ref, ...), custom_call_target="tpu_custom_call" | custom-call | flops 335544320 | bytes 6070276 | tf_op jit(solution)/shard_map/first/pallas_call | solution.py:465
  29.0 5.9 %all-to-all-start.1 = ((f32[32,1,1152]{2,1,0:T(1,128)}), f32[32,1,1152]{2,1,0:T(1,128)S(1)}, u32[]{:S(2)}, u32[]{:S(2)}) async-start(f32[32,1,1152]{2,1,0:T(1,128)} %get-tuple-element.36), calls=%async_computation.1 | async-start | bytes 294912 | tf_op jit(solution)/shard_map/all_to_all | solution.py:478
  34.9 7.8 %near1.1.image_ref = f32[16,2048]{1,0:T(8,128)S(1)} custom-call(f32[1]{0:T(128)S(6)} %copy.10.noise_ref, f32[16,2048]{1,0:T(8,128)S(1)} %get-tuple-element.37.vector_ref.w0_ref, bf16[256,9216]{1,0:T(8,128)(2,1)} %get-tuple-element.38.high_hbm, bf16[256,9216]{1,0:T(8,128)(2,1)} %get-tuple-element.39.low_hbm), custom_call_target="tpu_custom_call" | custom-call | flops 1073741824 | bytes 9699332 | tf_op jit(solution)/shard_map/near1/pallas_call | solution.py:465
  42.7 0.3 all-to-all-done.1.recv_ref
  43.1 0.0 copy-start
  43.1 3.5 %second.1 = (f32[16,2048]{1,0:T(8,128)S(1)}, f32[16,2048]{1,0:T(8,128)S(1)}, f32[16,128]{1,0:T(8,128)S(1)}, f32[32,1,1152]{2,1,0:T(1,128)}) custom-call(s32[1]{0:T(128)S(6)} %copy.9.sizes_ref, f32[32,1,1152]{2,1,0:T(1,128)S(1)} %all-to-all-done.1.recv_ref, f32[16,2048]{1,0:T(8,128)S(1)} %near1.1.image_ref, f32[16,2048]{1,0:T(8,128)S(1)} %get-tuple-element.40.q0_ref, ...), custom_call_target="tpu_custom_call" | custom-call | flops 335544320 | bytes 6209540 | tf_op jit(solution)/shard_map/second/pallas_call | solution.py:465
  46.6 5.3 %all-to-all-start.2 = ((f32[32,1,1152]{2,1,0:T(1,128)}), f32[32,1,1152]{2,1,0:T(1,128)S(1)}, u32[]{:S(2)}, u32[]{:S(2)}) async-start(f32[32,1,1152]{2,1,0:T(1,128)} %get-tuple-element.42), calls=%async_computation.2 | async-start | bytes 294912 | tf_op jit(solution)/shard_map/all_to_all | solution.py:478
  51.9 0.0 copy-done
  51.9 8.9 %near2.1 = (f32[16,2048]{1,0:T(8,128)S(1)}, s32[1,2048]{1,0:T(1,128)S(1)}) custom-call(f32[1]{0:T(128)S(6)} %copy.10.noise_ref, f32[16,2048]{1,0:T(8,128)S(1)} %get-tuple-element.43.vector_ref.w1_ref, bf16[256,9216]{1,0:T(8,128)(2,1)} %get-tuple-element.38.high_hbm, bf16[256,9216]{1,0:T(8,128)(2,1)} %get-tuple-element.39.low_hbm, s32[1,2048]{1,0:T(1,128)S(1)} %copy-done), custom_call_target="tpu_custom_call" | custom-call | flops 1073741824 | bytes 9715716 | tf_op jit(solution)/shard_map/near2/pallas_call | solution.py:465
  60.8 0.0 all-to-all-done.2.recv_ref
  60.8 0.9 %third.1 = (f32[16,2048]{1,0:T(8,128)S(1)}, f32[16,128]{1,0:T(8,128)S(1)}, f32[32,1,128]{2,1,0:T(1,128)S(1)}) custom-call(s32[1]{0:T(128)S(6)} %copy.9.sizes_ref, f32[32,1,1152]{2,1,0:T(1,128)S(1)} %all-to-all-done.2.recv_ref, f32[16,2048]{1,0:T(8,128)S(1)} %get-tuple-element.44.image_ref, f32[16,2048]{1,0:T(8,128)S(1)} %get-tuple-element.40.q0_ref, ...), custom_call_target="tpu_custom_call" | custom-call | flops 335544320 | bytes 3588100 | tf_op jit(solution)/shard_map/third/pallas_call | solution.py:465
  61.7 12.8 %all_to_all.20.recv_ref = f32[32,1,128]{2,1,0:T(1,128)S(1)} all-to-all(f32[32,1,128]{2,1,0:T(1,128)S(1)} %get-tuple-element.47), channel_id=1, replica_groups=mesh['gx'=4,'gy'=8] {'gx','gy'}, dimensions={0} | all-to-all | bytes 32768 | tf_op jit(solution)/shard_map/all_to_all | solution.py:478
  74.5 2.6 %last.1 = f32[16,2048]{1,0:T(8,128)} custom-call(f32[32,1,128]{2,1,0:T(1,128)S(1)} %all_to_all.20.recv_ref, f32[16,2048]{1,0:T(8,128)S(1)} %get-tuple-element.40.q0_ref, f32[16,2048]{1,0:T(8,128)S(1)} %get-tuple-element.45.q1_ref, f32[16,2048]{1,0:T(8,128)S(1)} %get-tuple-element.48.q2_ref, f32[16,128]{1,0:T(8,128)S(1)} %get-tuple-element.49.old_ref, ...), custom_call_target="tpu_custom_call" | custom-call | flops 335544320 | bytes 557056 | tf_op jit(solution)/shard_map/last/pallas_call | solution.py:465
Async XLA Ops:
  0.7 0.7 copy-start.1
  7.0 17.8 %all-to-all-start = ((f32[32,1,1152]{2,1,0:T(1,128)}), f32[32,1,1152]{2,1,0:T(1,128)S(1)}, u32[]{:S(2)}, u32[]{:S(2)}) async-start(f32[32,1,1152]{2,1,0:T(1,128)} %get-tuple-element.28), calls=%async_computation | async-start | bytes 294912 | tf_op jit(solution)/shard_map/all_to_all | solution.py:478
  29.0 14.1 %all-to-all-start.1 = ((f32[32,1,1152]{2,1,0:T(1,128)}), f32[32,1,1152]{2,1,0:T(1,128)S(1)}, u32[]{:S(2)}, u32[]{:S(2)}) async-start(f32[32,1,1152]{2,1,0:T(1,128)} %get-tuple-element.36), calls=%async_computation.1 | async-start | bytes 294912 | tf_op jit(solution)/shard_map/all_to_all | solution.py:478
  43.1 8.8 %copy-start = (s32[1,2048]{1,0:T(1,128)S(1)}, s32[1,2048]{1,0:T(1,128)}, u32[]{:S(2)}) copy-start(s32[1,2048]{1,0:T(1,128)} %refs_0_.1) | copy-start | bytes 24580
  46.6 14.2 %all-to-all-start.2 = ((f32[32,1,1152]{2,1,0:T(1,128)}), f32[32,1,1152]{2,1,0:T(1,128)S(1)}, u32[]{:S(2)}, u32[]{:S(2)}) async-start(f32[32,1,1152]{2,1,0:T(1,128)} %get-tuple-element.42), calls=%async_computation.2 | async-start | bytes 294912 | tf_op jit(solution)/shard_map/all_to_all | solution.py:478

commit v3 on v2

--- a/solution.py
+++ b/solution.py
@@ -138,14 +138,20 @@
 
 
 def start_body(
-    sizes_ref, scales_ref, order_hbm, rhs_hbm, coords_hbm, v_hbm,
-    start_ref, points_ref, pay_ref, v1_hbm, v2_hbm,
-    order_ref, rhs_ref, coords_ref, pad_ref, v_ref, v1_ref, v2_ref, sem, *, levels, rank,
+    sizes_ref, scales_hbm, order_hbm, rhs_hbm, coords_hbm, v_hbm,
+    start_ref, points_ref, pay_ref,
+    scales_ref, order_ref, rhs_ref, coords_ref, pad_ref, v_ref, sem, *, levels, rank,
 ):
     loads = [
         pltpu.make_async_copy(source, target, sem.at[n])
         for n, (source, target) in enumerate(
-            [(order_hbm, order_ref), (rhs_hbm, rhs_ref), (coords_hbm, coords_ref), (v_hbm, v_ref)]
+            [
+                (scales_hbm, scales_ref),
+                (order_hbm, order_ref),
+                (rhs_hbm, rhs_ref),
+                (coords_hbm, coords_ref),
+                (v_hbm, v_ref),
+            ]
         )
     ]
     for load in loads:
@@ -153,7 +159,7 @@
     vectors, length = rhs_ref.shape
     dims = coords_ref.shape[0]
     pad_ref[...] = jnp.zeros(pad_ref.shape, f32)
-    for load in loads[:3]:
+    for load in loads[:4]:
         load.wait()
     pad_ref[:dims, :] = coords_ref[...]
     stacked = jnp.concatenate(
@@ -174,32 +180,39 @@
         rest = chosen[3 * vectors :]
         value = rest[:rows] + rest[rows : 2 * rows] + rest[2 * rows :]
         points_ref[:, base : base + TILE] = value * scale
-    loads[3].wait()
-    high, low = split(v_ref[...], 2)
-    v1_ref[...] = high
-    v2_ref[...] = low
-    stores = [
-        pltpu.make_async_copy(v1_ref, v1_hbm, sem.at[4]),
-        pltpu.make_async_copy(v2_ref, v2_hbm, sem.at[5]),
-    ]
-    for store in stores:
-        store.start()
-    start = start_ref[...]
-    dots = pack_dots([(start, start)], vectors)
-    send_coefs(start, high, low, pay_ref, dots, levels, rank)
-    for store in stores:
-        store.wait()
+
+    @stage(sizes_ref[0])
+    def _():
+        loads[4].wait()
+        high, low = split(v_ref[...], 2)
+        start = start_ref[...]
+        dots = pack_dots([(start, start)], vectors)
+        send_coefs(start, high, low, pay_ref, dots, levels, rank)
+
+
+def blocks_of(ref, first, count):
+    return jnp.concatenate(
+        [ref[(first + n) * TILE : (first + n + 1) * TILE, :] for n in range(count)], axis=1
+    )
+
+
+def stage(value):
+    return pl.when(value > -1)
 
 
 def add_panel(stacked, high_ref, low_ref, acc_ref, base, offset):
     width = acc_ref.shape[1] - base
     own = stacked[:, base : base + TILE]
+    first = offset // LANES
     for half in (high_ref, low_ref):
-        acc_ref[:, base:] += dot(own, half[:, offset : offset + width])
+        panel = blocks_of(half, first, width // LANES)
+        acc_ref[:, base:] += dot(own, panel)
         if width > TILE:
-            acc_ref[:, base : base + TILE] += dot_nt(
-                stacked[:, base + TILE :], half[:, offset + TILE : offset + width]
-            )
+            acc_ref[:, base : base + TILE] += dot_nt(stacked[:, base + TILE :], panel[:, TILE:])
+
+
+def panel_rows(ref, offset, width):
+    return ref.at[pl.ds(offset // LANES * TILE, width // LANES * TILE), :]
 
 
 def finish(acc_ref, noise_ref, vector):
@@ -243,25 +256,31 @@
                 distance = square * lax.rsqrt(square)
                 value = (1.0 / LN2 + distance) * jnp.exp2(-distance)
                 high, low = split(value, 2)
-                place = offset + lane - base
-                high_ref[row : row + step, place : place + LANES] = high
-                low_ref[row : row + step, place : place + LANES] = low
+                place = (offset + lane - base) // LANES * TILE + row
+                high_ref[place : place + step, :] = high
+                low_ref[place : place + step, :] = low
         for source, target in ((high_ref, high_hbm), (low_ref, low_hbm)):
             copy = pltpu.make_async_copy(
-                source.at[:, offset : offset + width],
-                target.at[:, offset : offset + width],
+                panel_rows(source, offset, width),
+                panel_rows(target, offset, width),
                 sem.at[1 + len(copies)],
             )
             copy.start()
             copies.append(copy)
         add_panel(stacked, high_ref, low_ref, acc_ref, base, offset)
     image_ref[...] = finish(acc_ref, noise_ref, start)
-    load.wait()
-    high, low = split(u_ref[...], 2)
-    u1_ref[...] = high
-    u2_ref[...] = low
-    for copy in copies:
-        copy.wait()
+
+    @stage(noise_ref[0])
+    def _():
+        load.wait()
+        high, low = split(u_ref[...], 2)
+        u1_ref[...] = high
+        u2_ref[...] = low
+
+    @stage(noise_ref[0])
+    def _():
+        for copy in copies:
+            copy.wait()
 
 
 def near_body(
@@ -277,20 +296,28 @@
     for base, offset, width in panels(length):
         for source, target in ((high_hbm, high_ref), (low_hbm, low_ref)):
             copy = pltpu.make_async_copy(
-                source.at[:, offset : offset + width],
-                target.at[:, offset : offset + width],
+                panel_rows(source, offset, width),
+                panel_rows(target, offset, width),
                 sem.at[len(copies)],
             )
-            copy.start()
             copies.append(copy)
+    ahead = 4
+    for copy in copies[:ahead]:
+        copy.start()
     stacked = jnp.concatenate(split(vector, 3), axis=0)
     acc_ref[...] = jnp.zeros(acc_ref.shape, f32)
     if order:
         inverse_ref[...] = inverse_of(order_ref)
     for number, (base, offset, width) in enumerate(panels(length)):
-        copies[2 * number].wait()
-        copies[2 * number + 1].wait()
-        add_panel(stacked, high_ref, low_ref, acc_ref, base, offset)
+
+        @stage(noise_ref[0])
+        def _(number=number, base=base, offset=offset):
+            for copy in copies[2 * number : 2 * number + 2]:
+                copy.wait()
+            for copy in copies[2 * number + ahead : 2 * number + ahead + 2]:
+                copy.start()
+            add_panel(stacked, high_ref, low_ref, acc_ref, base, offset)
+
     image_ref[...] = finish(acc_ref, noise_ref, vector)
 
 
@@ -306,21 +333,12 @@
     return (total[0:1] + total[1:2] * float(TILE)).astype(jnp.int32)
 
 
-def load_pair(high_hbm, low_hbm, high_ref, low_ref, sem):
-    loads = [
-        pltpu.make_async_copy(high_hbm, high_ref, sem.at[0]),
-        pltpu.make_async_copy(low_hbm, low_ref, sem.at[1]),
-    ]
-    for load in loads:
-        load.start()
-    return loads
-
-
 def first_body(
-    sizes_ref, recv_ref, image_ref, start_ref, u1_ref, u2_ref, v1_hbm, v2_hbm,
-    q0_ref, w0_ref, scal_ref, pay_ref, v1_ref, v2_ref, sem, *, levels, rank,
+    sizes_ref, recv_ref, image_ref, start_ref, u1_ref, u2_ref, v_hbm,
+    q0_ref, w0_ref, scal_ref, pay_ref, v_ref, sem, *, levels, rank,
 ):
-    loads = load_pair(v1_hbm, v2_hbm, v1_ref, v2_ref, sem)
+    load = pltpu.make_async_copy(v_hbm, v_ref, sem.at[0])
+    load.start()
     vectors, length = start_ref.shape
     live = live_row(sizes_ref[0], length)
     (norm,) = unpack_dots(recv_ref[:, 0, rank * vectors :], 1, vectors)
@@ -333,9 +351,12 @@
     w0_ref[...] = w0
     scal_ref[...] = jnp.broadcast_to(beta, scal_ref.shape)
     dots = pack_dots([(q0, q0), (q0, w0), (w0, w0)], vectors)
-    for load in loads:
+
+    @stage(sizes_ref[0])
+    def _():
         load.wait()
-    send_coefs(w0, v1_ref[...], v2_ref[...], pay_ref, dots, levels, rank)
+        high, low = split(v_ref[...], 2)
+        send_coefs(w0_ref[...], high, low, pay_ref, dots, levels, rank)
 
 
 def put_scalars(scal_ref, values):
@@ -351,10 +372,11 @@
 
 
 def second_body(
-    sizes_ref, recv_ref, image_ref, q0_ref, w0_ref, old_ref, u1_ref, u2_ref, v1_hbm, v2_hbm,
-    q1_ref, w1_ref, scal_ref, pay_ref, v1_ref, v2_ref, sem, *, levels, rank,
+    sizes_ref, recv_ref, image_ref, q0_ref, w0_ref, old_ref, u1_ref, u2_ref, v_hbm,
+    q1_ref, w1_ref, scal_ref, pay_ref, v_ref, sem, *, levels, rank,
 ):
-    loads = load_pair(v1_hbm, v2_hbm, v1_ref, v2_ref, sem)
+    load = pltpu.make_async_copy(v_hbm, v_ref, sem.at[0])
+    load.start()
     vectors, length = q0_ref.shape
     live = live_row(sizes_ref[0], length)
     (beta,) = get_scalars(old_ref, 1)
@@ -371,9 +393,12 @@
     q1_ref[...] = q1
     w1_ref[...] = w1
     dots = pack_dots([(q0, w1), (q1, w1), (w1, w1), (q0, q1), (q1, q1)], vectors)
-    for load in loads:
+
+    @stage(sizes_ref[0])
+    def _():
         load.wait()
-    send_coefs(w1, v1_ref[...], v2_ref[...], pay_ref, dots, levels, rank)
+        high, low = split(v_ref[...], 2)
+        send_coefs(w1_ref[...], high, low, pay_ref, dots, levels, rank)
 
 
 def third_body(
@@ -498,10 +523,9 @@
     factor = shaped(levels * rank, length, dtype=bf16)
     scalars = ("v", shaped(vectors, LANES))
     message = ("v", shaped(num, 1, rank * vectors + LANES))
-    panel = shaped(TILE, packed, dtype=bf16)
+    panel = shaped(packed // LANES * TILE, LANES, dtype=bf16)
     acc = pltpu.VMEM((3 * vectors, length), f32)
-    panel_space = pltpu.VMEM((TILE, packed), bf16)
-    factor_space = pltpu.VMEM((levels * rank, length), bf16)
+    panel_space = pltpu.VMEM((packed // LANES * TILE, LANES), bf16)
     whole_space = pltpu.VMEM((levels * rank, length), f32)
     sizes = dict(levels=levels, rank=rank)
     small = 2 * levels * rank * length * 256
@@ -509,20 +533,19 @@
     def arrays(memory, *values):
         return [(memory, value) for value in values]
 
-    start, points, pay, v1, v2 = call(
+    start, points, pay = call(
         functools.partial(start_body, **sizes),
-        [field, ("v", shaped(padded, length)), message, ("h", factor), ("h", factor)],
-        arrays("s", leaf_sizes, inverse_scales)
-        + arrays("h", leaf_order, rhs, coordinates, v_flat),
+        [field, ("v", shaped(padded, length)), message],
+        arrays("s", leaf_sizes)
+        + arrays("h", inverse_scales, leaf_order, rhs, coordinates, v_flat),
         scratch=[
+            pltpu.SMEM((dims,), f32),
             pltpu.VMEM((1, length), jnp.int32),
             pltpu.VMEM((vectors, length), f32),
             pltpu.VMEM((dims, length), f32),
             pltpu.VMEM((padded, length), f32),
             whole_space,
-            factor_space,
-            factor_space,
-            pltpu.SemaphoreType.DMA((6,)),
+            pltpu.SemaphoreType.DMA((5,)),
         ],
         flops=small, name="start",
     )
@@ -552,12 +575,12 @@
             flops=2 * length * length * 128, limit=30000, name=name,
         )
 
-    pair_space = [factor_space, factor_space, pltpu.SemaphoreType.DMA((2,))]
+    whole_load = [whole_space, pltpu.SemaphoreType.DMA((1,))]
     q0, w0, scal, pay = call(
         functools.partial(first_body, **sizes),
         [field, field, scalars, message],
-        arrays("s", leaf_sizes) + arrays("v", recv, image, start, u1, u2) + arrays("h", v1, v2),
-        scratch=pair_space, flops=small, name="first",
+        arrays("s", leaf_sizes) + arrays("v", recv, image, start, u1, u2) + arrays("h", v_flat),
+        scratch=whole_load, flops=small, name="first",
     )
     recv = exchange(pay)
     (image,) = near(w0, "near1", False)
@@ -565,8 +588,8 @@
         functools.partial(second_body, **sizes),
         [field, field, scalars, message],
         arrays("s", leaf_sizes) + arrays("v", recv, image, q0, w0, scal, u1, u2)
-        + arrays("h", v1, v2),
-        scratch=pair_space, flops=small, name="second",
+        + arrays("h", v_flat),
+        scratch=whole_load, flops=small, name="second",
     )
     recv = exchange(pay)
     image, inverse = near(w1, "near2", True)

time: 77.5 us -> 70.9 us (0.915)
  Pallas kernels: 43.2 us -> 37.1 us
  waiting for transfers between devices: 0.35 us -> 2.64 us
  starting transfers between devices: 18.7 us -> 17.4 us
  blocking collectives: 12.8 us -> 11.8 us
    pallas_call x8, Pallas kernels: 43.2 us -> 37.1 us  [call(): pl.pallas_call(body, out_shape=[pltpu.HBM(a.shape, a.dtype) if m == 'h' e...]
    all_to_all x3, waiting for transfers between devices: 0.35 us -> 2.64 us  [exchange(): return lax.all_to_all(payload, AXES, 0, 0, tiled=True)]
    all_to_all x3, starting transfers between devices: 18.7 us -> 17.4 us  [exchange(): return lax.all_to_all(payload, AXES, 0, 0, tiled=True)]
    all_to_all x1, blocking collectives: 12.8 us -> 11.8 us  [exchange(): return lax.all_to_all(payload, AXES, 0, 0, tiled=True)]
  transfers between devices with their start and end apart: 3 -> 3, of which waited for: 1 -> 2; matrix products, arithmetic and copies ran while one was open for 0% -> 0% of each run, Pallas kernels for 34% -> 32%
where the time goes in v3:
time: 70.9 us; the launch traced here: 70.4 us
  Pallas kernels  37.1 us (52%)
  starting transfers between devices  17.4 us (25%)
  blocking collectives  11.8 us (17%)
  waiting for transfers between devices  2.64 us (4%)
  between operations  1.4 us (2%)
    pallas_call x8, Pallas kernels, call(): pl.pallas_call(body, out_shape=[pltpu.HBM(a.shape, a.dtype) if m == 'h' e...  37.1 us
    all_to_all x3, starting transfers between devices, exchange(): return lax.all_to_all(payload, AXES, 0, 0, tiled=True)  17.4 us
    all_to_all x1, blocking collectives, exchange(): return lax.all_to_all(payload, AXES, 0, 0, tiled=True)  11.8 us
    all_to_all x3, waiting for transfers between devices, exchange(): return lax.all_to_all(payload, AXES, 0, 0, tiled=True)  2.64 us
  transfers between devices with their start and end apart: 3, of which 2 were waited for; matrix products, arithmetic and copies ran while one was open for 0% of the time, Pallas kernels for 32%

profile of v3, /device:TPU:0, one launch (start us, length us, event | category | flops | bytes accessed | tf_op | source)
XLA Modules:
  0.0 70.4 jit_solution(17190042505422988204)
XLA Ops:
  0.7 4.0 %start.1 = (f32[16,2048]{1,0:T(8,128)S(1)}, f32[8,2048]{1,0:T(8,128)S(1)}, f32[32,1,1152]{2,1,0:T(1,128)}) custom-call(s32[1]{0:T(128)S(6)} %copy.9.sizes_ref, f32[3]{0:T(128)} %scales_hbm.1, s32[1,2048]{1,0:T(1,128)} %refs_0_.1, f32[16,2048]{1,0:T(8,128)} %rhs_hbm.1, f32[3,2048]{1,0:T(4,128)} %coords_hbm.1, f32[320,2048]{1,0:T(8,128)} %bitcast.2), custom_call_target="tpu_custom_call" | custom-call | flops 335544320 | bytes 3129360 | tf_op jit(solution)/shard_map/start/pallas_call | solution.py:490
  4.6 7.3 %all-to-all-start = ((f32[32,1,1152]{2,1,0:T(1,128)}), f32[32,1,1152]{2,1,0:T(1,128)S(1)}, u32[]{:S(2)}, u32[]{:S(2)}) async-start(f32[32,1,1152]{2,1,0:T(1,128)} %get-tuple-element.26), calls=%async_computation | async-start | bytes 294912 | tf_op jit(solution)/shard_map/all_to_all | solution.py:503
  12.6 8.6 %build.1 = (bf16[18432,128]{1,0:T(8,128)(2,1)}, bf16[18432,128]{1,0:T(8,128)(2,1)}, f32[16,2048]{1,0:T(8,128)S(1)}, bf16[320,2048]{1,0:T(8,128)(2,1)S(1)}, bf16[320,2048]{1,0:T(8,128)(2,1)S(1)}) custom-call(f32[1]{0:T(128)S(6)} %copy.10.noise_ref, f32[8,2048]{1,0:T(8,128)S(1)} %get-tuple-element.27.points_ref, f32[16,2048]{1,0:T(8,128)S(1)} %get-tuple-element.28.start_ref, ...), custom_call_target="tpu_custom_call" | custom-call | flops 2147483648 | bytes 15007748 | tf_op jit(solution)/shard_map/build/pallas_call | solution.py:490
  21.2 0.0 all-to-all-done.recv_ref
  21.2 3.5 %first.1 = (f32[16,2048]{1,0:T(8,128)S(1)}, f32[16,2048]{1,0:T(8,128)S(1)}, f32[16,128]{1,0:T(8,128)S(1)}, f32[32,1,1152]{2,1,0:T(1,128)}) custom-call(s32[1]{0:T(128)S(6)} %copy.9.sizes_ref, f32[32,1,1152]{2,1,0:T(1,128)S(1)} %all-to-all-done.recv_ref, f32[16,2048]{1,0:T(8,128)S(1)} %get-tuple-element.29.image_ref, ...), custom_call_target="tpu_custom_call" | custom-call | flops 335544320 | bytes 6070276 | tf_op jit(solution)/shard_map/first/pallas_call | solution.py:490
  24.7 5.8 %all-to-all-start.1 = ((f32[32,1,1152]{2,1,0:T(1,128)}), f32[32,1,1152]{2,1,0:T(1,128)S(1)}, u32[]{:S(2)}, u32[]{:S(2)}) async-start(f32[32,1,1152]{2,1,0:T(1,128)} %get-tuple-element.32), calls=%async_computation.1 | async-start | bytes 294912 | tf_op jit(solution)/shard_map/all_to_all | solution.py:503
  30.5 6.8 %near1.1.image_ref = f32[16,2048]{1,0:T(8,128)S(1)} custom-call(f32[1]{0:T(128)S(6)} %copy.10.noise_ref, f32[16,2048]{1,0:T(8,128)S(1)} %get-tuple-element.33.vector_ref.w0_ref, bf16[18432,128]{1,0:T(8,128)(2,1)} %get-tuple-element.34.high_hbm, bf16[18432,128]{1,0:T(8,128)(2,1)} %get-tuple-element.35.low_hbm), custom_call_target="tpu_custom_call" | custom-call | flops 1073741824 | bytes 9699332 | tf_op jit(solution)/shard_map/near1/pallas_call | solution.py:490
  37.3 1.6 %all-to-all-done.1.recv_ref = f32[32,1,1152]{2,1,0:T(1,128)S(1)} async-done(((f32[32,1,1152]{2,1,0:T(1,128)}), f32[32,1,1152]{2,1,0:T(1,128)S(1)}, u32[]{:S(2)}, u32[]{:S(2)}) %all-to-all-start.1) | async-done | bytes 147488 | tf_op jit(solution)/shard_map/all_to_all | solution.py:503
  38.9 0.0 copy-start
  38.9 3.5 %second.1 = (f32[16,2048]{1,0:T(8,128)S(1)}, f32[16,2048]{1,0:T(8,128)S(1)}, f32[16,128]{1,0:T(8,128)S(1)}, f32[32,1,1152]{2,1,0:T(1,128)}) custom-call(s32[1]{0:T(128)S(6)} %copy.9.sizes_ref, f32[32,1,1152]{2,1,0:T(1,128)S(1)} %all-to-all-done.1.recv_ref, f32[16,2048]{1,0:T(8,128)S(1)} %near1.1.image_ref, f32[16,2048]{1,0:T(8,128)S(1)} %get-tuple-element.36.q0_ref, ...), custom_call_target="tpu_custom_call" | custom-call | flops 335544320 | bytes 6209540 | tf_op jit(solution)/shard_map/second/pallas_call | solution.py:490
  42.4 4.3 %all-to-all-start.2 = ((f32[32,1,1152]{2,1,0:T(1,128)}), f32[32,1,1152]{2,1,0:T(1,128)S(1)}, u32[]{:S(2)}, u32[]{:S(2)}) async-start(f32[32,1,1152]{2,1,0:T(1,128)} %get-tuple-element.38), calls=%async_computation.2 | async-start | bytes 294912 | tf_op jit(solution)/shard_map/all_to_all | solution.py:503
  46.7 0.0 copy-done
  46.7 7.4 %near2.1 = (f32[16,2048]{1,0:T(8,128)S(1)}, s32[1,2048]{1,0:T(1,128)S(1)}) custom-call(f32[1]{0:T(128)S(6)} %copy.10.noise_ref, f32[16,2048]{1,0:T(8,128)S(1)} %get-tuple-element.39.vector_ref.w1_ref, bf16[18432,128]{1,0:T(8,128)(2,1)} %get-tuple-element.34.high_hbm, bf16[18432,128]{1,0:T(8,128)(2,1)} %get-tuple-element.35.low_hbm, s32[1,2048]{1,0:T(1,128)S(1)} %copy-done), custom_call_target="tpu_custom_call" | custom-call | flops 1073741824 | bytes 9715716 | tf_op jit(solution)/shard_map/near2/pallas_call | solution.py:490
  54.0 1.0 %all-to-all-done.2.recv_ref = f32[32,1,1152]{2,1,0:T(1,128)S(1)} async-done(((f32[32,1,1152]{2,1,0:T(1,128)}), f32[32,1,1152]{2,1,0:T(1,128)S(1)}, u32[]{:S(2)}, u32[]{:S(2)}) %all-to-all-start.2) | async-done | bytes 147488 | tf_op jit(solution)/shard_map/all_to_all | solution.py:503
  55.1 0.9 %third.1 = (f32[16,2048]{1,0:T(8,128)S(1)}, f32[16,128]{1,0:T(8,128)S(1)}, f32[32,1,128]{2,1,0:T(1,128)S(1)}) custom-call(s32[1]{0:T(128)S(6)} %copy.9.sizes_ref, f32[32,1,1152]{2,1,0:T(1,128)S(1)} %all-to-all-done.2.recv_ref, f32[16,2048]{1,0:T(8,128)S(1)} %get-tuple-element.40.image_ref, f32[16,2048]{1,0:T(8,128)S(1)} %get-tuple-element.36.q0_ref, ...), custom_call_target="tpu_custom_call" | custom-call | flops 335544320 | bytes 3588100 | tf_op jit(solution)/shard_map/third/pallas_call | solution.py:490
  56.0 11.8 %all_to_all.20.recv_ref = f32[32,1,128]{2,1,0:T(1,128)S(1)} all-to-all(f32[32,1,128]{2,1,0:T(1,128)S(1)} %get-tuple-element.43), channel_id=1, replica_groups=mesh['gx'=4,'gy'=8] {'gx','gy'}, dimensions={0} | all-to-all | bytes 32768 | tf_op jit(solution)/shard_map/all_to_all | solution.py:503
  67.8 2.6 %last.1 = f32[16,2048]{1,0:T(8,128)} custom-call(f32[32,1,128]{2,1,0:T(1,128)S(1)} %all_to_all.20.recv_ref, f32[16,2048]{1,0:T(8,128)S(1)} %get-tuple-element.36.q0_ref, f32[16,2048]{1,0:T(8,128)S(1)} %get-tuple-element.41.q1_ref, f32[16,2048]{1,0:T(8,128)S(1)} %get-tuple-element.44.q2_ref, f32[16,128]{1,0:T(8,128)S(1)} %get-tuple-element.45.old_ref, ...), custom_call_target="tpu_custom_call" | custom-call | flops 335544320 | bytes 557056 | tf_op jit(solution)/shard_map/last/pallas_call | solution.py:490
Async XLA Ops:
  4.6 16.5 %all-to-all-start = ((f32[32,1,1152]{2,1,0:T(1,128)}), f32[32,1,1152]{2,1,0:T(1,128)S(1)}, u32[]{:S(2)}, u32[]{:S(2)}) async-start(f32[32,1,1152]{2,1,0:T(1,128)} %get-tuple-element.26), calls=%async_computation | async-start | bytes 294912 | tf_op jit(solution)/shard_map/all_to_all | solution.py:503
  24.7 14.3 %all-to-all-start.1 = ((f32[32,1,1152]{2,1,0:T(1,128)}), f32[32,1,1152]{2,1,0:T(1,128)S(1)}, u32[]{:S(2)}, u32[]{:S(2)}) async-start(f32[32,1,1152]{2,1,0:T(1,128)} %get-tuple-element.32), calls=%async_computation.1 | async-start | bytes 294912 | tf_op jit(solution)/shard_map/all_to_all | solution.py:503
  38.9 7.7 %copy-start = (s32[1,2048]{1,0:T(1,128)S(1)}, s32[1,2048]{1,0:T(1,128)}, u32[]{:S(2)}) copy-start(s32[1,2048]{1,0:T(1,128)} %refs_0_.1) | copy-start | bytes 24580
  42.4 12.7 %all-to-all-start.2 = ((f32[32,1,1152]{2,1,0:T(1,128)}), f32[32,1,1152]{2,1,0:T(1,128)S(1)}, u32[]{:S(2)}, u32[]{:S(2)}) async-start(f32[32,1,1152]{2,1,0:T(1,128)} %get-tuple-element.38), calls=%async_computation.2 | async-start | bytes 294912 | tf_op jit(solution)/shard_map/all_to_all | solution.py:503

commit v4 on v3

--- a/solution.py
+++ b/solution.py
@@ -34,6 +34,10 @@
 
 def dot_nt(a, b):
     return lax.dot_general(a, b, (((1,), (1,)), ((), ())), preferred_element_type=f32)
+
+
+def dot_halves(a, high, low):
+    return dot(jnp.concatenate([a, a], axis=1), jnp.concatenate([high, low], axis=0))
 
 
 def live_row(size, length):
@@ -138,7 +142,7 @@
 
 
 def start_body(
-    sizes_ref, scales_hbm, order_hbm, rhs_hbm, coords_hbm, v_hbm,
+    sizes_ref, noise_ref, scales_hbm, order_hbm, rhs_hbm, coords_hbm, v_hbm,
     start_ref, points_ref, pay_ref,
     scales_ref, order_ref, rhs_ref, coords_ref, pad_ref, v_ref, sem, *, levels, rank,
 ):
@@ -179,7 +183,7 @@
         start_ref[:, base : base + TILE] = jnp.where(lane < sizes_ref[0], value, 0.0)
         rest = chosen[3 * vectors :]
         value = rest[:rows] + rest[rows : 2 * rows] + rest[2 * rows :]
-        points_ref[:, base : base + TILE] = value * scale
+        points_ref[:, base : base + TILE] = jnp.where(row_id == dims, noise_ref[0], value * scale)
 
     @stage(sizes_ref[0])
     def _():
@@ -204,22 +208,26 @@
     width = acc_ref.shape[1] - base
     own = stacked[:, base : base + TILE]
     first = offset // LANES
-    for half in (high_ref, low_ref):
-        panel = blocks_of(half, first, width // LANES)
-        acc_ref[:, base:] += dot(own, panel)
-        if width > TILE:
-            acc_ref[:, base : base + TILE] += dot_nt(stacked[:, base + TILE :], panel[:, TILE:])
+    high = blocks_of(high_ref, first, width // LANES)
+    low = blocks_of(low_ref, first, width // LANES)
+    acc_ref[:, base:] += dot_halves(own, high, low)
+    if width > TILE:
+        rest = stacked[:, base + TILE :]
+        acc_ref[:, base : base + TILE] += dot_nt(
+            jnp.concatenate([rest, rest], axis=1),
+            jnp.concatenate([high[:, TILE:], low[:, TILE:]], axis=1),
+        )
 
 
 def panel_rows(ref, offset, width):
     return ref.at[pl.ds(offset // LANES * TILE, width // LANES * TILE), :]
 
 
-def finish(acc_ref, noise_ref, vector):
+def finish(acc_ref, points_ref, vector, dims):
     vectors = vector.shape[0]
     out = acc_ref[...]
     out = out[:vectors] + out[vectors : 2 * vectors] + out[2 * vectors :]
-    return LN2 * out + noise_ref[0] * vector
+    return LN2 * out + points_ref[dims : dims + 1, :] * vector
 
 
 def panels(length):
@@ -230,7 +238,7 @@
 
 
 def build_body(
-    noise_ref, points_ref, start_ref, u_hbm, high_hbm, low_hbm, image_ref, u1_ref, u2_ref,
+    sizes_ref, points_ref, start_ref, u_hbm, high_hbm, low_hbm, image_ref, u1_ref, u2_ref,
     u_ref, wide_ref, high_ref, low_ref, acc_ref, sem, *, dims,
 ):
     length = points_ref.shape[1]
@@ -268,28 +276,25 @@
             copy.start()
             copies.append(copy)
         add_panel(stacked, high_ref, low_ref, acc_ref, base, offset)
-    image_ref[...] = finish(acc_ref, noise_ref, start)
-
-    @stage(noise_ref[0])
+
+    @stage(sizes_ref[0])
     def _():
+        image_ref[...] = finish(acc_ref, points_ref, start, dims)
         load.wait()
         high, low = split(u_ref[...], 2)
         u1_ref[...] = high
         u2_ref[...] = low
 
-    @stage(noise_ref[0])
+    @stage(sizes_ref[0])
     def _():
         for copy in copies:
             copy.wait()
 
 
 def near_body(
-    noise_ref, vector_ref, high_hbm, low_hbm, *refs, order
+    sizes_ref, points_ref, vector_ref, high_hbm, low_hbm, image_ref,
+    high_ref, low_ref, acc_ref, sem, *, dims,
 ):
-    if order:
-        order_ref, image_ref, inverse_ref, high_ref, low_ref, acc_ref, sem = refs
-    else:
-        image_ref, high_ref, low_ref, acc_ref, sem = refs
     vector = vector_ref[...]
     length = vector.shape[1]
     copies = []
@@ -306,11 +311,9 @@
         copy.start()
     stacked = jnp.concatenate(split(vector, 3), axis=0)
     acc_ref[...] = jnp.zeros(acc_ref.shape, f32)
-    if order:
-        inverse_ref[...] = inverse_of(order_ref)
     for number, (base, offset, width) in enumerate(panels(length)):
 
-        @stage(noise_ref[0])
+        @stage(sizes_ref[0])
         def _(number=number, base=base, offset=offset):
             for copy in copies[2 * number : 2 * number + 2]:
                 copy.wait()
@@ -318,19 +321,27 @@
                 copy.start()
             add_panel(stacked, high_ref, low_ref, acc_ref, base, offset)
 
-    image_ref[...] = finish(acc_ref, noise_ref, vector)
-
-
-def inverse_of(order_ref):
-    length = order_ref.shape[1]
-    place = lax.broadcasted_iota(jnp.int32, (8, TILE), 1).astype(f32)
-    row_id = lax.broadcasted_iota(jnp.int32, (8, TILE), 0)
-    total = jnp.zeros((8, length), f32)
+    @stage(sizes_ref[0])
+    def _():
+        image_ref[...] = finish(acc_ref, points_ref, vector, dims)
+
+
+def place_body(order_ref, *refs):
+    count = (len(refs) - 1) // 2
+    sources, targets, acc_ref = refs[:count], refs[count : 2 * count], refs[-1]
+    vectors, length = sources[0].shape
+    stacked = jnp.concatenate([p for ref in sources for p in split(ref[...], 3)], axis=0)
     for base in range(0, length, TILE):
-        weights = jnp.where(row_id == 0, place, float(base // TILE))
         hot = one_hot(order_ref[:, base : base + TILE], length)
-        total = total + dot_nt(weights.astype(bf16), hot)
-    return (total[0:1] + total[1:2] * float(TILE)).astype(jnp.int32)
+        part = dot_nt(stacked[:, base : base + TILE], hot)
+        if base == 0:
+            acc_ref[...] = part
+        else:
+            acc_ref[...] += part
+    for number, target in enumerate(targets):
+        first = 3 * number * vectors
+        pieces = [acc_ref[first + n * vectors : first + (n + 1) * vectors, :] for n in range(3)]
+        target[...] = pieces[0] + pieces[1] + pieces[2]
 
 
 def first_body(
@@ -403,7 +414,7 @@
 
 def third_body(
     sizes_ref, recv_ref, image_ref, q0_ref, q1_ref, w0_ref, w1_ref, old_ref, u1_ref, u2_ref,
-    q2_ref, scal_ref, pay_ref, *, levels, rank,
+    scal_ref, pay_ref, *, levels, rank,
 ):
     vectors, length = q0_ref.shape
     live = live_row(sizes_ref[0], length)
@@ -424,7 +435,6 @@
     q2 = (w1 - h01 * q0 - h11 * q1) * inverse
     image = jnp.where(live, image_ref[...] + distant, 0.0)
     w2 = (image - h01 * w0 - h11 * w1) * inverse
-    q2_ref[...] = q2
     dots = pack_dots(
         [(q0, w2), (q1, w2), (q2, w2), (w2, w2), (q0, q2), (q1, q2), (q2, q2)], vectors
     )
@@ -464,7 +474,7 @@
     return weights
 
 
-def last_body(recv_ref, q0_ref, q1_ref, q2_ref, old_ref, inverse_ref, out_ref):
+def last_body(recv_ref, q0_ref, q1_ref, w1_ref, old_ref, out_ref):
     vectors, length = q0_ref.shape
     beta, g00, h00, h10, g01, g11, h01, h11, h21 = get_scalars(old_ref, 9)
     h02, h12, h22, norm, g02, g12, g22 = unpack_dots(recv_ref[:, 0, :], 7, vectors)
@@ -475,13 +485,10 @@
     )
     h32 = jnp.sqrt(jnp.maximum(rest, 0.0) + EPSILON)
     y0, y1, y2 = least_squares([[h00, h10], [h01, h11, h21], [h02, h12, h22, h32]], beta)
-    solved = y0 * q0_ref[...] + y1 * q1_ref[...] + y2 * q2_ref[...]
-    stacked = jnp.concatenate(split(solved, 3), axis=0)
-    for base in range(0, length, TILE):
-        placed = dot(stacked, one_hot(inverse_ref[:, base : base + TILE], length))
-        out_ref[:, base : base + TILE] = (
-            placed[:vectors] + placed[vectors : 2 * vectors] + placed[2 * vectors :]
-        )
+    q0 = q0_ref[...]
+    q1 = q1_ref[...]
+    q2 = (w1_ref[...] - h01 * q0 - h11 * q1) * (1.0 / h21)
+    out_ref[...] = y0 * q0 + y1 * q1 + y2 * q2
 
 
 def call(body, outs, args, scratch=(), flops=0, limit=20000, name=None):
@@ -512,7 +519,7 @@
     num = lax.axis_size("gx") * lax.axis_size("gy")
     blocks = length // TILE
     packed = TILE * (blocks * (blocks + 1) // 2)
-    padded = -(-dims // 8) * 8
+    padded = dims // 8 * 8 + 8
     u_flat = u_factors.reshape(levels * rank, length)
     v_flat = v_factors.reshape(levels * rank, length)
 
@@ -536,7 +543,7 @@
     start, points, pay = call(
         functools.partial(start_body, **sizes),
         [field, ("v", shaped(padded, length)), message],
-        arrays("s", leaf_sizes)
+        arrays("s", leaf_sizes, noise_var)
         + arrays("h", inverse_scales, leaf_order, rhs, coordinates, v_flat),
         scratch=[
             pltpu.SMEM((dims,), f32),
@@ -553,7 +560,7 @@
     k1, k2, image, u1, u2 = call(
         functools.partial(build_body, dims=dims),
         [("h", panel), ("h", panel), field, ("v", factor), ("v", factor)],
-        arrays("s", noise_var) + arrays("v", points, start) + arrays("h", u_flat),
+        arrays("s", leaf_sizes) + arrays("v", points, start) + arrays("h", u_flat),
         scratch=[
             whole_space,
             pltpu.VMEM((dims, length, LANES), f32),
@@ -565,15 +572,20 @@
         flops=2 * length * length * 256, limit=40000, name="build",
     )
 
-    def near(vector, name, order):
-        return call(
-            functools.partial(near_body, order=order),
-            [field] + ([("v", shaped(1, length, dtype=jnp.int32))] if order else []),
-            arrays("s", noise_var) + arrays("v", vector) + arrays("h", k1, k2)
-            + (arrays("v", leaf_order) if order else []),
-            scratch=[panel_space, panel_space, acc, pltpu.SemaphoreType.DMA((2 * blocks,))],
+    def near(vector, name):
+        (out,) = call(
+            functools.partial(near_body, dims=dims), [field],
+            arrays("s", leaf_sizes) + arrays("v", points, vector)
+            + arrays("h", k1, k2),
+            scratch=[
+                panel_space,
+                panel_space,
+                acc,
+                pltpu.SemaphoreType.DMA((2 * blocks,)),
+            ],
             flops=2 * length * length * 128, limit=30000, name=name,
         )
+        return out
 
     whole_load = [whole_space, pltpu.SemaphoreType.DMA((1,))]
     q0, w0, scal, pay = call(
@@ -583,7 +595,7 @@
         scratch=whole_load, flops=small, name="first",
     )
     recv = exchange(pay)
-    (image,) = near(w0, "near1", False)
+    image = near(w0, "near1")
     q1, w1, scal, pay = call(
         functools.partial(second_body, **sizes),
         [field, field, scalars, message],
@@ -592,16 +604,21 @@
         scratch=whole_load, flops=small, name="second",
     )
     recv = exchange(pay)
-    image, inverse = near(w1, "near2", True)
-    q2, scal, pay = call(
+    image = near(w1, "near2")
+    scal, pay = call(
         functools.partial(third_body, **sizes),
-        [field, scalars, ("v", shaped(num, 1, LANES))],
+        [scalars, ("v", shaped(num, 1, LANES))],
         arrays("s", leaf_sizes) + arrays("v", recv, image, q0, q1, w0, w1, scal, u1, u2),
         flops=small, name="third",
     )
     recv = exchange(pay)
+    placed = call(
+        place_body, [field] * 3, arrays("v", leaf_order, q0, q1, w1),
+        scratch=[pltpu.VMEM((9 * vectors, length), f32)],
+        flops=2 * length * length * 128, name="place",
+    )
     (out,) = call(
-        last_body, [field], arrays("v", recv, q0, q1, q2, scal, inverse), flops=small, name="last"
+        last_body, [field], arrays("v", recv, *placed, scal), flops=small, name="last"
     )
     return out
 

time: 70.9 us -> 69.6 us (0.982)
  blocking collectives: 11.8 us -> 0 us
  waiting for transfers between devices: 2.64 us -> 7.69 us
  starting transfers between devices: 17.4 us -> 21.8 us
  Pallas kernels: 37.1 us -> 38.2 us
    all_to_all x1 -> x0, blocking collectives: 11.8 us -> none  [exchange(): return lax.all_to_all(payload, AXES, 0, 0, tiled=True)]
    all_to_all x3 -> x4, waiting for transfers between devices: 2.64 us -> 7.69 us  [exchange(): return lax.all_to_all(payload, AXES, 0, 0, tiled=True)]
    all_to_all x3 -> x4, starting transfers between devices: 17.4 us -> 21.8 us  [exchange(): return lax.all_to_all(payload, AXES, 0, 0, tiled=True)]
    pallas_call x8 -> x9, Pallas kernels: 37.1 us -> 38.2 us  [call(): pl.pallas_call(body, out_shape=[pltpu.HBM(a.shape, a.dtype) if m == 'h' e...]
  transfers between devices with their start and end apart: 3 -> 4, of which waited for: 2 -> 3; matrix products, arithmetic and copies ran while one was open for 0% -> 0% of each run, Pallas kernels for 32% -> 36%
where the time goes in v4:
time: 69.6 us; the launch traced here: 69.1 us
  Pallas kernels  38.2 us (55%)
  starting transfers between devices  21.8 us (31%)
  waiting for transfers between devices  7.69 us (11%)
  between operations  1.4 us (2%)
    pallas_call x9, Pallas kernels, call(): pl.pallas_call(body, out_shape=[pltpu.HBM(a.shape, a.dtype) if m == 'h' e...  38.2 us
    all_to_all x4, starting transfers between devices, exchange(): return lax.all_to_all(payload, AXES, 0, 0, tiled=True)  21.8 us
    all_to_all x4, waiting for transfers between devices, exchange(): return lax.all_to_all(payload, AXES, 0, 0, tiled=True)  7.69 us
  transfers between devices with their start and end apart: 4, of which 3 were waited for; matrix products, arithmetic and copies ran while one was open for 0% of the time, Pallas kernels for 36%

profile of v4, /device:TPU:0, one launch (start us, length us, event | category | flops | bytes accessed | tf_op | source)
XLA Modules:
  0.0 69.1 jit_solution(10913247895878974005)
XLA Ops:
  1.3 4.0 %start.1 = (f32[16,2048]{1,0:T(8,128)S(1)}, f32[8,2048]{1,0:T(8,128)S(1)}, f32[32,1,1152]{2,1,0:T(1,128)}) custom-call(s32[1]{0:T(128)S(6)} %copy.9.sizes_ref, f32[1]{0:T(128)S(6)} %copy.10.noise_ref, f32[3]{0:T(128)} %scales_hbm.1, s32[1,2048]{1,0:T(1,128)} %order_ref.1, f32[16,2048]{1,0:T(8,128)} %rhs_hbm.1, f32[3,2048]{1,0:T(4,128)} %coords_hbm.1, ...), custom_call_target="tpu_custom_call" | custom-call | flops 335544320 | bytes 3129364 | tf_op jit(solution)/shard_map/start/pallas_call | solution.py:497
  5.3 7.3 %all-to-all-start = ((f32[32,1,1152]{2,1,0:T(1,128)}), f32[32,1,1152]{2,1,0:T(1,128)S(1)}, u32[]{:S(2)}, u32[]{:S(2)}) async-start(f32[32,1,1152]{2,1,0:T(1,128)} %get-tuple-element.26), calls=%async_computation | async-start | bytes 294912 | tf_op jit(solution)/shard_map/all_to_all | solution.py:510
  12.6 8.4 %build.1 = (bf16[18432,128]{1,0:T(8,128)(2,1)}, bf16[18432,128]{1,0:T(8,128)(2,1)}, f32[16,2048]{1,0:T(8,128)S(1)}, bf16[320,2048]{1,0:T(8,128)(2,1)S(1)}, bf16[320,2048]{1,0:T(8,128)(2,1)S(1)}) custom-call(s32[1]{0:T(128)S(6)} %copy.9.sizes_ref, f32[8,2048]{1,0:T(8,128)S(1)} %get-tuple-element.27.points_ref, f32[16,2048]{1,0:T(8,128)S(1)} %get-tuple-element.28.start_ref, ...), custom_call_target="tpu_custom_call" | custom-call | flops 2147483648 | bytes 15007748 | tf_op jit(solution)/shard_map/build/pallas_call | solution.py:497
  21.0 0.0 all-to-all-done.recv_ref
  21.1 3.5 %first.1 = (f32[16,2048]{1,0:T(8,128)S(1)}, f32[16,2048]{1,0:T(8,128)S(1)}, f32[16,128]{1,0:T(8,128)S(1)}, f32[32,1,1152]{2,1,0:T(1,128)}) custom-call(s32[1]{0:T(128)S(6)} %copy.9.sizes_ref, f32[32,1,1152]{2,1,0:T(1,128)S(1)} %all-to-all-done.recv_ref, f32[16,2048]{1,0:T(8,128)S(1)} %get-tuple-element.29.image_ref, ...), custom_call_target="tpu_custom_call" | custom-call | flops 335544320 | bytes 6070276 | tf_op jit(solution)/shard_map/first/pallas_call | solution.py:497
  24.5 5.8 %all-to-all-start.1 = ((f32[32,1,1152]{2,1,0:T(1,128)}), f32[32,1,1152]{2,1,0:T(1,128)S(1)}, u32[]{:S(2)}, u32[]{:S(2)}) async-start(f32[32,1,1152]{2,1,0:T(1,128)} %get-tuple-element.32), calls=%async_computation.1 | async-start | bytes 294912 | tf_op jit(solution)/shard_map/all_to_all | solution.py:510
  30.4 6.9 %near1.1.image_ref = f32[16,2048]{1,0:T(8,128)S(1)} custom-call(s32[1]{0:T(128)S(6)} %copy.9.sizes_ref, f32[8,2048]{1,0:T(8,128)S(1)} %get-tuple-element.27.points_ref, f32[16,2048]{1,0:T(8,128)S(1)} %get-tuple-element.33.vector_ref.w0_ref, bf16[18432,128]{1,0:T(8,128)(2,1)} %get-tuple-element.34.high_hbm, bf16[18432,128]{1,0:T(8,128)(2,1)} %get-tuple-element.35.low_hbm), custom_call_target="tpu_custom_call" | custom-call | flops 1073741824 | bytes 9764868 | tf_op jit(solution)/shard_map/near1/pallas_call | solution.py:497
  37.3 1.5 %all-to-all-done.1.recv_ref = f32[32,1,1152]{2,1,0:T(1,128)S(1)} async-done(((f32[32,1,1152]{2,1,0:T(1,128)}), f32[32,1,1152]{2,1,0:T(1,128)S(1)}, u32[]{:S(2)}, u32[]{:S(2)}) %all-to-all-start.1) | async-done | bytes 147488 | tf_op jit(solution)/shard_map/all_to_all | solution.py:510
  38.8 3.5 %second.1 = (f32[16,2048]{1,0:T(8,128)S(1)}, f32[16,2048]{1,0:T(8,128)S(1)}, f32[16,128]{1,0:T(8,128)S(1)}, f32[32,1,1152]{2,1,0:T(1,128)}) custom-call(s32[1]{0:T(128)S(6)} %copy.9.sizes_ref, f32[32,1,1152]{2,1,0:T(1,128)S(1)} %all-to-all-done.1.recv_ref, f32[16,2048]{1,0:T(8,128)S(1)} %near1.1.image_ref, f32[16,2048]{1,0:T(8,128)S(1)} %get-tuple-element.36.q0_ref.refs_0_, ...), custom_call_target="tpu_custom_call" | custom-call | flops 335544320 | bytes 6209540 | tf_op jit(solution)/shard_map/second/pallas_call | solution.py:497
  42.2 4.4 %all-to-all-start.2 = ((f32[32,1,1152]{2,1,0:T(1,128)}), f32[32,1,1152]{2,1,0:T(1,128)S(1)}, u32[]{:S(2)}, u32[]{:S(2)}) async-start(f32[32,1,1152]{2,1,0:T(1,128)} %get-tuple-element.38), calls=%async_computation.2 | async-start | bytes 294912 | tf_op jit(solution)/shard_map/all_to_all | solution.py:510
  46.7 6.8 %near2.1.image_ref = f32[16,2048]{1,0:T(8,128)S(1)} custom-call(s32[1]{0:T(128)S(6)} %copy.9.sizes_ref, f32[8,2048]{1,0:T(8,128)S(1)} %get-tuple-element.27.points_ref, f32[16,2048]{1,0:T(8,128)S(1)} %get-tuple-element.39.vector_ref.w1_ref.refs_2_, bf16[18432,128]{1,0:T(8,128)(2,1)} %get-tuple-element.34.high_hbm, bf16[18432,128]{1,0:T(8,128)(2,1)} %get-tuple-element.35.low_hbm), custom_call_target="tpu_custom_call" | custom-call | flops 1073741824 | bytes 9764868 | tf_op jit(solution)/shard_map/near2/pallas_call | solution.py:497
  53.4 0.0 copy-start
  53.4 1.6 %all-to-all-done.2.recv_ref = f32[32,1,1152]{2,1,0:T(1,128)S(1)} async-done(((f32[32,1,1152]{2,1,0:T(1,128)}), f32[32,1,1152]{2,1,0:T(1,128)S(1)}, u32[]{:S(2)}, u32[]{:S(2)}) %all-to-all-start.2) | async-done | bytes 147488 | tf_op jit(solution)/shard_map/all_to_all | solution.py:510
  55.1 1.5 %third.1 = (f32[16,128]{1,0:T(8,128)S(1)}, f32[32,1,128]{2,1,0:T(1,128)}) custom-call(s32[1]{0:T(128)S(6)} %copy.9.sizes_ref, f32[32,1,1152]{2,1,0:T(1,128)S(1)} %all-to-all-done.2.recv_ref, f32[16,2048]{1,0:T(8,128)S(1)} %near2.1.image_ref, f32[16,2048]{1,0:T(8,128)S(1)} %get-tuple-element.36.q0_ref.refs_0_, ...), custom_call_target="tpu_custom_call" | custom-call | flops 335544320 | bytes 3457028 | tf_op jit(solution)/shard_map/third/pallas_call | solution.py:497
  56.6 4.2 %all-to-all-start.3 = ((f32[32,1,128]{2,1,0:T(1,128)}), f32[32,1,128]{2,1,0:T(1,128)S(1)}, u32[]{:S(2)}, u32[]{:S(2)}) async-start(f32[32,1,128]{2,1,0:T(1,128)} %get-tuple-element.42), calls=%async_computation.3 | async-start | bytes 32768 | tf_op jit(solution)/shard_map/all_to_all | solution.py:510
  60.8 0.0 copy-done
  60.8 2.5 %place.1 = (f32[16,2048]{1,0:T(8,128)S(1)}, f32[16,2048]{1,0:T(8,128)S(1)}, f32[16,2048]{1,0:T(8,128)S(1)}) custom-call(s32[1,2048]{1,0:T(1,128)S(1)} %copy-done, f32[16,2048]{1,0:T(8,128)S(1)} %get-tuple-element.36.q0_ref.refs_0_, f32[16,2048]{1,0:T(8,128)S(1)} %get-tuple-element.40.q1_ref.refs_1_, f32[16,2048]{1,0:T(8,128)S(1)} %get-tuple-element.39.vector_ref.w1_ref.refs_2_), custom_call_target="tpu_custom_call" | custom-call | flops 1073741824 | bytes 794624 | tf_op jit(solution)/shard_map/place/pallas_call | solution.py:497
  63.3 4.6 %all-to-all-done.3.recv_ref = f32[32,1,128]{2,1,0:T(1,128)S(1)} async-done(((f32[32,1,128]{2,1,0:T(1,128)}), f32[32,1,128]{2,1,0:T(1,128)S(1)}, u32[]{:S(2)}, u32[]{:S(2)}) %all-to-all-start.3) | async-done | bytes 16416 | tf_op jit(solution)/shard_map/all_to_all | solution.py:510
  67.9 1.2 %last.1 = f32[16,2048]{1,0:T(8,128)} custom-call(f32[32,1,128]{2,1,0:T(1,128)S(1)} %all-to-all-done.3.recv_ref, f32[16,2048]{1,0:T(8,128)S(1)} %get-tuple-element.43.q0_ref, f32[16,2048]{1,0:T(8,128)S(1)} %get-tuple-element.44.q1_ref, f32[16,2048]{1,0:T(8,128)S(1)} %get-tuple-element.45.w1_ref, f32[16,128]{1,0:T(8,128)S(1)} %get-tuple-element.46.old_ref), custom_call_target="tpu_custom_call" | custom-call | flops 335544320 | bytes 548864 | tf_op jit(solution)/shard_map/last/pallas_call | solution.py:497
Async XLA Ops:
  5.3 15.8 %all-to-all-start = ((f32[32,1,1152]{2,1,0:T(1,128)}), f32[32,1,1152]{2,1,0:T(1,128)S(1)}, u32[]{:S(2)}, u32[]{:S(2)}) async-start(f32[32,1,1152]{2,1,0:T(1,128)} %get-tuple-element.26), calls=%async_computation | async-start | bytes 294912 | tf_op jit(solution)/shard_map/all_to_all | solution.py:510
  24.5 14.3 %all-to-all-start.1 = ((f32[32,1,1152]{2,1,0:T(1,128)}), f32[32,1,1152]{2,1,0:T(1,128)S(1)}, u32[]{:S(2)}, u32[]{:S(2)}) async-start(f32[32,1,1152]{2,1,0:T(1,128)} %get-tuple-element.32), calls=%async_computation.1 | async-start | bytes 294912 | tf_op jit(solution)/shard_map/all_to_all | solution.py:510
  42.2 12.8 %all-to-all-start.2 = ((f32[32,1,1152]{2,1,0:T(1,128)}), f32[32,1,1152]{2,1,0:T(1,128)S(1)}, u32[]{:S(2)}, u32[]{:S(2)}) async-start(f32[32,1,1152]{2,1,0:T(1,128)} %get-tuple-element.38), calls=%async_computation.2 | async-start | bytes 294912 | tf_op jit(solution)/shard_map/all_to_all | solution.py:510
  53.4 7.4 %copy-start = (s32[1,2048]{1,0:T(1,128)S(1)}, s32[1,2048]{1,0:T(1,128)}, u32[]{:S(2)}) copy-start(s32[1,2048]{1,0:T(1,128)} %order_ref.1) | copy-start | bytes 24580
  56.6 11.3 %all-to-all-start.3 = ((f32[32,1,128]{2,1,0:T(1,128)}), f32[32,1,128]{2,1,0:T(1,128)S(1)}, u32[]{:S(2)}, u32[]{:S(2)}) async-start(f32[32,1,128]{2,1,0:T(1,128)} %get-tuple-element.42), calls=%async_computation.3 | async-start | bytes 32768 | tf_op jit(solution)/shard_map/all_to_all | solution.py:510

commit v5 on v4

--- a/solution.py
+++ b/solution.py
@@ -306,7 +306,7 @@
                 sem.at[len(copies)],
             )
             copies.append(copy)
-    ahead = 4
+    ahead = 6
     for copy in copies[:ahead]:
         copy.start()
     stacked = jnp.concatenate(split(vector, 3), axis=0)

time: 69.6 us -> 68.9 us (0.990)
  transfers between devices with their start and end apart: 4 -> 4, of which waited for: 3 -> 3; matrix products, arithmetic and copies ran while one was open for 0% -> 0% of each run, Pallas kernels for 36% -> 35%
where the time goes in v5:
time: 68.9 us; the launch traced here: 68.6 us
  Pallas kernels  37.7 us (55%)
  starting transfers between devices  21.2 us (31%)
  waiting for transfers between devices  8.25 us (12%)
  between operations  1.4 us (2%)
    pallas_call x9, Pallas kernels, call(): pl.pallas_call(body, out_shape=[pltpu.HBM(a.shape, a.dtype) if m == 'h' e...  37.7 us
    all_to_all x4, starting transfers between devices, exchange(): return lax.all_to_all(payload, AXES, 0, 0, tiled=True)  21.2 us
    all_to_all x4, waiting for transfers between devices, exchange(): return lax.all_to_all(payload, AXES, 0, 0, tiled=True)  8.25 us
  transfers between devices with their start and end apart: 4, of which 3 were waited for; matrix products, arithmetic and copies ran while one was open for 0% of the time, Pallas kernels for 35%

profile of v5, /device:TPU:0, one launch (start us, length us, event | category | flops | bytes accessed | tf_op | source)
XLA Modules:
  0.0 68.6 jit_solution(493800837444840399)
XLA Ops:
  1.3 4.0 %start.1 = (f32[16,2048]{1,0:T(8,128)S(1)}, f32[8,2048]{1,0:T(8,128)S(1)}, f32[32,1,1152]{2,1,0:T(1,128)}) custom-call(s32[1]{0:T(128)S(6)} %copy.9.sizes_ref, f32[1]{0:T(128)S(6)} %copy.10.noise_ref, f32[3]{0:T(128)} %scales_hbm.1, s32[1,2048]{1,0:T(1,128)} %order_ref.1, f32[16,2048]{1,0:T(8,128)} %rhs_hbm.1, f32[3,2048]{1,0:T(4,128)} %coords_hbm.1, ...), custom_call_target="tpu_custom_call" | custom-call | flops 335544320 | bytes 3129364 | tf_op jit(solution)/shard_map/start/pallas_call | solution.py:497
  5.3 7.3 %all-to-all-start = ((f32[32,1,1152]{2,1,0:T(1,128)}), f32[32,1,1152]{2,1,0:T(1,128)S(1)}, u32[]{:S(2)}, u32[]{:S(2)}) async-start(f32[32,1,1152]{2,1,0:T(1,128)} %get-tuple-element.26), calls=%async_computation | async-start | bytes 294912 | tf_op jit(solution)/shard_map/all_to_all | solution.py:510
  12.6 8.4 %build.1 = (bf16[18432,128]{1,0:T(8,128)(2,1)}, bf16[18432,128]{1,0:T(8,128)(2,1)}, f32[16,2048]{1,0:T(8,128)S(1)}, bf16[320,2048]{1,0:T(8,128)(2,1)S(1)}, bf16[320,2048]{1,0:T(8,128)(2,1)S(1)}) custom-call(s32[1]{0:T(128)S(6)} %copy.9.sizes_ref, f32[8,2048]{1,0:T(8,128)S(1)} %get-tuple-element.27.points_ref, f32[16,2048]{1,0:T(8,128)S(1)} %get-tuple-element.28.start_ref, ...), custom_call_target="tpu_custom_call" | custom-call | flops 2147483648 | bytes 15007748 | tf_op jit(solution)/shard_map/build/pallas_call | solution.py:497
  21.0 0.0 all-to-all-done.recv_ref
  21.1 3.5 %first.1 = (f32[16,2048]{1,0:T(8,128)S(1)}, f32[16,2048]{1,0:T(8,128)S(1)}, f32[16,128]{1,0:T(8,128)S(1)}, f32[32,1,1152]{2,1,0:T(1,128)}) custom-call(s32[1]{0:T(128)S(6)} %copy.9.sizes_ref, f32[32,1,1152]{2,1,0:T(1,128)S(1)} %all-to-all-done.recv_ref, f32[16,2048]{1,0:T(8,128)S(1)} %get-tuple-element.29.image_ref, ...), custom_call_target="tpu_custom_call" | custom-call | flops 335544320 | bytes 6070276 | tf_op jit(solution)/shard_map/first/pallas_call | solution.py:497
  24.5 5.8 %all-to-all-start.1 = ((f32[32,1,1152]{2,1,0:T(1,128)}), f32[32,1,1152]{2,1,0:T(1,128)S(1)}, u32[]{:S(2)}, u32[]{:S(2)}) async-start(f32[32,1,1152]{2,1,0:T(1,128)} %get-tuple-element.32), calls=%async_computation.1 | async-start | bytes 294912 | tf_op jit(solution)/shard_map/all_to_all | solution.py:510
  30.4 6.7 %near1.1.image_ref = f32[16,2048]{1,0:T(8,128)S(1)} custom-call(s32[1]{0:T(128)S(6)} %copy.9.sizes_ref, f32[8,2048]{1,0:T(8,128)S(1)} %get-tuple-element.27.points_ref, f32[16,2048]{1,0:T(8,128)S(1)} %get-tuple-element.33.vector_ref.w0_ref, bf16[18432,128]{1,0:T(8,128)(2,1)} %get-tuple-element.34.high_hbm, bf16[18432,128]{1,0:T(8,128)(2,1)} %get-tuple-element.35.low_hbm), custom_call_target="tpu_custom_call" | custom-call | flops 1073741824 | bytes 9764868 | tf_op jit(solution)/shard_map/near1/pallas_call | solution.py:497
  37.0 1.7 %all-to-all-done.1.recv_ref = f32[32,1,1152]{2,1,0:T(1,128)S(1)} async-done(((f32[32,1,1152]{2,1,0:T(1,128)}), f32[32,1,1152]{2,1,0:T(1,128)S(1)}, u32[]{:S(2)}, u32[]{:S(2)}) %all-to-all-start.1) | async-done | bytes 147488 | tf_op jit(solution)/shard_map/all_to_all | solution.py:510
  38.8 3.5 %second.1 = (f32[16,2048]{1,0:T(8,128)S(1)}, f32[16,2048]{1,0:T(8,128)S(1)}, f32[16,128]{1,0:T(8,128)S(1)}, f32[32,1,1152]{2,1,0:T(1,128)}) custom-call(s32[1]{0:T(128)S(6)} %copy.9.sizes_ref, f32[32,1,1152]{2,1,0:T(1,128)S(1)} %all-to-all-done.1.recv_ref, f32[16,2048]{1,0:T(8,128)S(1)} %near1.1.image_ref, f32[16,2048]{1,0:T(8,128)S(1)} %get-tuple-element.36.q0_ref.refs_0_, ...), custom_call_target="tpu_custom_call" | custom-call | flops 335544320 | bytes 6209540 | tf_op jit(solution)/shard_map/second/pallas_call | solution.py:497
  42.2 4.1 %all-to-all-start.2 = ((f32[32,1,1152]{2,1,0:T(1,128)}), f32[32,1,1152]{2,1,0:T(1,128)S(1)}, u32[]{:S(2)}, u32[]{:S(2)}) async-start(f32[32,1,1152]{2,1,0:T(1,128)} %get-tuple-element.38), calls=%async_computation.2 | async-start | bytes 294912 | tf_op jit(solution)/shard_map/all_to_all | solution.py:510
  46.4 6.5 %near2.1.image_ref = f32[16,2048]{1,0:T(8,128)S(1)} custom-call(s32[1]{0:T(128)S(6)} %copy.9.sizes_ref, f32[8,2048]{1,0:T(8,128)S(1)} %get-tuple-element.27.points_ref, f32[16,2048]{1,0:T(8,128)S(1)} %get-tuple-element.39.vector_ref.w1_ref.refs_2_, bf16[18432,128]{1,0:T(8,128)(2,1)} %get-tuple-element.34.high_hbm, bf16[18432,128]{1,0:T(8,128)(2,1)} %get-tuple-element.35.low_hbm), custom_call_target="tpu_custom_call" | custom-call | flops 1073741824 | bytes 9764868 | tf_op jit(solution)/shard_map/near2/pallas_call | solution.py:497
  52.9 0.0 copy-start
  52.9 1.9 %all-to-all-done.2.recv_ref = f32[32,1,1152]{2,1,0:T(1,128)S(1)} async-done(((f32[32,1,1152]{2,1,0:T(1,128)}), f32[32,1,1152]{2,1,0:T(1,128)S(1)}, u32[]{:S(2)}, u32[]{:S(2)}) %all-to-all-start.2) | async-done | bytes 147488 | tf_op jit(solution)/shard_map/all_to_all | solution.py:510
  54.8 1.5 %third.1 = (f32[16,128]{1,0:T(8,128)S(1)}, f32[32,1,128]{2,1,0:T(1,128)}) custom-call(s32[1]{0:T(128)S(6)} %copy.9.sizes_ref, f32[32,1,1152]{2,1,0:T(1,128)S(1)} %all-to-all-done.2.recv_ref, f32[16,2048]{1,0:T(8,128)S(1)} %near2.1.image_ref, f32[16,2048]{1,0:T(8,128)S(1)} %get-tuple-element.36.q0_ref.refs_0_, ...), custom_call_target="tpu_custom_call" | custom-call | flops 335544320 | bytes 3457028 | tf_op jit(solution)/shard_map/third/pallas_call | solution.py:497
  56.3 3.9 %all-to-all-start.3 = ((f32[32,1,128]{2,1,0:T(1,128)}), f32[32,1,128]{2,1,0:T(1,128)S(1)}, u32[]{:S(2)}, u32[]{:S(2)}) async-start(f32[32,1,128]{2,1,0:T(1,128)} %get-tuple-element.42), calls=%async_computation.3 | async-start | bytes 32768 | tf_op jit(solution)/shard_map/all_to_all | solution.py:510
  60.3 0.0 copy-done
  60.3 2.5 %place.1 = (f32[16,2048]{1,0:T(8,128)S(1)}, f32[16,2048]{1,0:T(8,128)S(1)}, f32[16,2048]{1,0:T(8,128)S(1)}) custom-call(s32[1,2048]{1,0:T(1,128)S(1)} %copy-done, f32[16,2048]{1,0:T(8,128)S(1)} %get-tuple-element.36.q0_ref.refs_0_, f32[16,2048]{1,0:T(8,128)S(1)} %get-tuple-element.40.q1_ref.refs_1_, f32[16,2048]{1,0:T(8,128)S(1)} %get-tuple-element.39.vector_ref.w1_ref.refs_2_), custom_call_target="tpu_custom_call" | custom-call | flops 1073741824 | bytes 794624 | tf_op jit(solution)/shard_map/place/pallas_call | solution.py:497
  62.8 4.6 %all-to-all-done.3.recv_ref = f32[32,1,128]{2,1,0:T(1,128)S(1)} async-done(((f32[32,1,128]{2,1,0:T(1,128)}), f32[32,1,128]{2,1,0:T(1,128)S(1)}, u32[]{:S(2)}, u32[]{:S(2)}) %all-to-all-start.3) | async-done | bytes 16416 | tf_op jit(solution)/shard_map/all_to_all | solution.py:510
  67.4 1.2 %last.1 = f32[16,2048]{1,0:T(8,128)} custom-call(f32[32,1,128]{2,1,0:T(1,128)S(1)} %all-to-all-done.3.recv_ref, f32[16,2048]{1,0:T(8,128)S(1)} %get-tuple-element.43.q0_ref, f32[16,2048]{1,0:T(8,128)S(1)} %get-tuple-element.44.q1_ref, f32[16,2048]{1,0:T(8,128)S(1)} %get-tuple-element.45.w1_ref, f32[16,128]{1,0:T(8,128)S(1)} %get-tuple-element.46.old_ref), custom_call_target="tpu_custom_call" | custom-call | flops 335544320 | bytes 548864 | tf_op jit(solution)/shard_map/last/pallas_call | solution.py:497
Async XLA Ops:
  5.3 15.8 %all-to-all-start = ((f32[32,1,1152]{2,1,0:T(1,128)}), f32[32,1,1152]{2,1,0:T(1,128)S(1)}, u32[]{:S(2)}, u32[]{:S(2)}) async-start(f32[32,1,1152]{2,1,0:T(1,128)} %get-tuple-element.26), calls=%async_computation | async-start | bytes 294912 | tf_op jit(solution)/shard_map/all_to_all | solution.py:510
  24.5 14.3 %all-to-all-start.1 = ((f32[32,1,1152]{2,1,0:T(1,128)}), f32[32,1,1152]{2,1,0:T(1,128)S(1)}, u32[]{:S(2)}, u32[]{:S(2)}) async-start(f32[32,1,1152]{2,1,0:T(1,128)} %get-tuple-element.32), calls=%async_computation.1 | async-start | bytes 294912 | tf_op jit(solution)/shard_map/all_to_all | solution.py:510
  42.2 12.5 %all-to-all-start.2 = ((f32[32,1,1152]{2,1,0:T(1,128)}), f32[32,1,1152]{2,1,0:T(1,128)S(1)}, u32[]{:S(2)}, u32[]{:S(2)}) async-start(f32[32,1,1152]{2,1,0:T(1,128)} %get-tuple-element.38), calls=%async_computation.2 | async-start | bytes 294912 | tf_op jit(solution)/shard_map/all_to_all | solution.py:510
  52.9 7.4 %copy-start = (s32[1,2048]{1,0:T(1,128)S(1)}, s32[1,2048]{1,0:T(1,128)}, u32[]{:S(2)}) copy-start(s32[1,2048]{1,0:T(1,128)} %order_ref.1) | copy-start | bytes 24580
  56.3 11.0 %all-to-all-start.3 = ((f32[32,1,128]{2,1,0:T(1,128)}), f32[32,1,128]{2,1,0:T(1,128)S(1)}, u32[]{:S(2)}, u32[]{:S(2)}) async-start(f32[32,1,128]{2,1,0:T(1,128)} %get-tuple-element.42), calls=%async_computation.3 | async-start | bytes 32768 | tf_op jit(solution)/shard_map/all_to_all | solution.py:510
